TPU v7x, 256 devices: a whole 4x4x8 slice. The times are simulated.
256 devices in a mesh: rep: 32 (over x, z_lo, y), shard: 8 (over z_hi, core).
Axes of the slice: x: 4, y: 4, z: 8 (z_hi: 4, z_lo: 2; z = z_hi * 2 + z_lo), core: 2. Of those that a mesh axis runs over, the one named last changes fastest.
Arguments:
- params: float32 [32, 1600, 3200], P('rep', None, 'shard'), may hold values from -6 to 6
- momentum: float32 [32, 1600, 3200], P('rep', None, 'shard'), may hold values from -6 to 6
- tokens: bfloat16 [32, 2, 1024, 1600], P('rep', None, 'shard'), may hold values from -6 to 6
- targets: bfloat16 [32, 2, 1024, 3200], P('rep', None, None, 'shard'), may hold values from -6 to 6
- blend_weight: float32 [3200], P('shard'), may hold values from 0.2 to 0.9
Outputs:
- averaged: float32 [1600, 3200], P(None, 'shard')
- blended: float32 [32, 1600, 3200], P('rep', None, 'shard')
All inputs are finite; a program needn't handle non-finite values.
Results may differ from a plain program's by a relative error of at most 0.0045.
Values may be sent and summed in bfloat16 or wider, within the bound.
No kernel may reach another device: no remote copies, remote signals or barrier semaphores. Data moves between devices by JAX's collectives and lax.ppermute only.
A program may use at most 128 MiB of HBM per device.

v0:
```python
import math

import jax
import jax.numpy as jnp
from jax import lax
from jax.experimental import pallas as pl
from jax.experimental.pallas import tpu as pltpu
from jax.sharding import PartitionSpec as P


D = 1600
TOP = D // 2
LANES = 128
SCALE = 1.0 / math.sqrt(D)
LEARN = 0.05
DECAY = 0.9


def rotated(up, cores):
    return [(2 * z + c, 2 * ((z + up) % 4) + (c + cores) % 2) for z in range(4) for c in range(2)]


def slope(pre, wanted):
    k = math.sqrt(2.0 / math.pi)
    square = pre * pre
    th = jnp.tanh(k * (pre + 0.044715 * pre * square))
    half = 0.5 * (1.0 + th)
    deriv = half + 0.5 * pre * (1.0 - th * th) * (k * (1.0 + 3 * 0.044715 * square))
    return (pre * half - wanted) * deriv * SCALE


def places(me, ups):
    z, c = me // 2, me % 2
    return [2 * ((z + up) % 4) + (c + k) % 2 for k in range(2) for up in ups]


def partial_gradient(step, at, weight, wanted, blocks, x):
    for i, (top, bottom) in enumerate(blocks):
        x[:TOP, i * LANES : (i + 1) * LANES] = top[...]
        x[TOP:, i * LANES : (i + 1) * LANES] = bottom[...]
    pre = jnp.dot(weight, x[...], preferred_element_type=jnp.float32) * SCALE
    want = jnp.concatenate(
        [wanted[step, :, pl.ds(pl.multiple_of(a * LANES, LANES), LANES)] for a in at], axis=1
    )
    hidden = slope(pre, want.astype(jnp.float32)).astype(jnp.bfloat16)
    return lax.dot_general(hidden, x[...], (((1,), (1,)), ((), ())), preferred_element_type=jnp.float32)


def pairs(refs):
    return [(refs[i], refs[i + 1]) for i in range(0, len(refs), 2)]


def early_kernel(step):
    def kernel(me, weight, wanted, *refs):
        *blocks, out, x = refs
        at = places(me[0], (0, 3, 1))
        out[...] = partial_gradient(step, at, weight[...].astype(jnp.bfloat16), wanted, pairs(blocks), x)

    return kernel


UNITS = 80
LINES = 1024
FULL = D // LANES


def pack(lines, value):
    for j in range(FULL):
        lines[j * UNITS : (j + 1) * UNITS, :] = value[:, j * LANES : (j + 1) * LANES].astype(jnp.bfloat16)
    rest = value[:, FULL * LANES :]
    folded = jnp.concatenate([rest[: UNITS // 2], rest[UNITS // 2 :]], axis=1)
    at = FULL * UNITS
    lines[at : at + UNITS // 2, :] = folded.astype(jnp.bfloat16)
    at += UNITS // 2
    lines[at:, :] = jnp.zeros((LINES - at, LANES), jnp.bfloat16)


def unpacked(lines, at):
    for j in range(FULL):
        yield slice(j * LANES, (j + 1) * LANES), lines[pl.ds(at + j * UNITS, UNITS), :].astype(jnp.float32)
    rest = lines[pl.ds(at + FULL * UNITS, UNITS // 2), :].astype(jnp.float32)
    half = LANES // 2
    yield slice(FULL * LANES, D), jnp.concatenate([rest[:, :half], rest[:, half:]], axis=0)


def late_kernel(step):
    def kernel(me, weight, wanted, grad, moment, *refs):
        count = 3 if step == 0 else 2
        blocks, refs = refs[:4], refs[4:]
        outs, bufs, (x, g, done) = refs[:count], refs[count : 2 * count], refs[2 * count :]
        at = places(me[0], (2,))
        g[...] = partial_gradient(step, at, weight[...].astype(jnp.bfloat16), wanted, pairs(blocks), x)
        copies = []
        for i in range(weight.shape[0] // UNITS):
            rows = slice(i * UNITS, (i + 1) * UNITS)
            taken = [slice(i * LINES, (i + 1) * LINES), rows, rows][:count]
            m = DECAY * moment[rows, :] + (grad[rows, :] + g[rows, :])
            bufs[1][rows, :] = m
            if step == 0:
                m = weight[rows, :] - LEARN * m
                bufs[2][rows, :] = m.astype(jnp.bfloat16)
            pack(bufs[0].at[taken[0], :], m)
            for k in range(count):
                copy = pltpu.make_async_copy(bufs[k].at[taken[k], :], outs[k].at[taken[k], :], done.at[k, i])
                copy.start()
                copies.append(copy)
        for copy in copies:
            copy.wait()

    return kernel


def last_kernel(blend, lines, mean_weight, moment, averaged, blended):
    b = blend[...]
    for lanes, m in unpacked(lines, pl.multiple_of(pl.program_id(0) * LINES, LINES)):
        averaged[:, lanes] = mean_weight[:, lanes].astype(jnp.float32) - LEARN * m
        blended[:, lanes] = b * m + (1.0 - b) * moment[:, lanes]


ROUND = (0, 3, 1, 2)


def spread_kernel(me, *refs):
    *parts, out, lines = refs
    x, y, core = me[0] // 8, me[0] % 4, me[1] % 2
    rows = lines.shape[0] // 16
    for part, far in zip(parts, ROUND):
        for i, near in enumerate(ROUND):
            dx, dy = near + core * (far - near), far + core * (near - far)
            owner = (x + dy) % 4 * 4 + (y + dx) % 4
            lines[pl.ds(pl.multiple_of(owner * rows, rows), rows), :] = part[i * rows : (i + 1) * rows, :]
    for u in range(out.shape[0] // UNITS):
        for lanes, v in unpacked(lines, u * LINES):
            out[u * UNITS : (u + 1) * UNITS, lanes] = v.astype(jnp.bfloat16)


SMEM = pl.BlockSpec(memory_space=pltpu.SMEM)
VMEM = pl.BlockSpec(memory_space=pltpu.VMEM)
MIB = 1 << 20


def call(kernel, outs, args, blocks, late):
    tokens, units = LANES * len(blocks) // 2, args[1].shape[0]
    scratch = [pltpu.VMEM((D, tokens), jnp.bfloat16)]
    if late:
        scratch = [pltpu.VMEM(o.shape, o.dtype) for o in outs] + scratch + [pltpu.VMEM((units, D), jnp.float32)]
        scratch.append(pltpu.SemaphoreType.DMA((len(outs), units // UNITS)))
    return pl.pallas_call(
        kernel,
        out_shape=tuple(pltpu.HBM(o.shape, o.dtype) for o in outs) if late else outs,
        in_specs=[SMEM] + [VMEM] * (len(args) - 1 + len(blocks)),
        out_specs=(pl.BlockSpec(memory_space=pltpu.HBM),) * len(outs) if late else VMEM,
        scratch_shapes=scratch,
        cost_estimate=pl.CostEstimate(
            flops=4 * tokens * units * D, bytes_accessed=8 * units * D, transcendentals=tokens * units
        ),
        compiler_params=pltpu.CompilerParams(vmem_limit_bytes=24 * MIB),
    )(*args, *blocks)


def gate_kernel(me, out):
    out[0] = me[0]


def gate(me):
    return pl.pallas_call(
        gate_kernel,
        out_shape=jax.ShapeDtypeStruct((1,), jnp.int32),
        in_specs=[SMEM],
        out_specs=SMEM,
        compiler_params=pltpu.CompilerParams(vmem_limit_bytes=MIB),
    )(me)


def shard_permute(v, up, cores):
    return lax.ppermute(v, "shard", rotated(up, cores))


def gather(piece):
    top, bottom = piece
    low_top = shard_permute(top, 1, 0)
    high_bottom = shard_permute(bottom, -1, 0)
    low_bottom = shard_permute(bottom, 1, 0)
    high_top = shard_permute(top, -1, 0)
    far_top = shard_permute(low_top, 1, 0)
    far_bottom = shard_permute(high_bottom, -1, 0)
    near = [top, bottom, low_top, low_bottom, high_top, high_bottom]
    return near, [far_top, far_bottom], (low_top, high_bottom)


def other_core(values):
    return [shard_permute(v, 0, 1) for v in values]


def added(got):
    return jnp.sum(got[...].astype(jnp.float32), axis=0)


def sum_kernel(got, out):
    out[...] = added(got).astype(jnp.bfloat16)


def mean_kernel(got, out):
    mean = (added(got) / got.shape[0]).astype(jnp.bfloat16)
    out[...] = jnp.broadcast_to(mean[None], out.shape)


def pair_kernel(here, there, out):
    out[...] = ((here[...].astype(jnp.float32) + there[...].astype(jnp.float32)) / 32).astype(jnp.bfloat16)


def small(kernel, args, shape):
    return pl.pallas_call(
        kernel,
        out_shape=jax.ShapeDtypeStruct(shape, jnp.bfloat16),
        in_specs=[VMEM] * len(args),
        out_specs=VMEM,
        compiler_params=pltpu.CompilerParams(vmem_limit_bytes=8 * MIB),
    )(*args)


def join_kernel(*refs):
    *parts, out = refs
    at = 0
    for part in parts:
        out[at : at + part.shape[0], :] = part[...]
        at += part.shape[0]


def replica_permute(v, core0, core1):
    pairs = []
    for r in range(32):
        for k in range(8):
            x, z, y = (core0, core1)[k % 2]
            to = 8 * ((r // 8 + x) % 4) + 4 * ((r // 4 + z) % 2) + (r + y) % 4
            pairs.append((8 * r + k, 8 * to + k))
    return lax.ppermute(v, ("rep", "shard"), pairs)


def weight_mean(lines):
    planes = [[8 * x + 4 * z + y for x in range(4) for y in range(4)] for z in range(2)]
    got = lax.all_to_all(lines.reshape(16, -1, LANES), "rep", 0, 0, axis_index_groups=planes)
    part = got.shape[1:]
    here = small(sum_kernel, [got], part)
    there = replica_permute(here, (0, 1, 0), (0, 1, 0))
    chunk = small(pair_kernel, [here, there], part)
    line = [replica_permute(chunk, (0, 0, k), (k, 0, 0)) for k in (1, 3, 2)]
    plane = small(join_kernel, [chunk, *line], (4 * part[0], LANES))
    return [plane] + [replica_permute(plane, (k, 0, 0), (0, 0, k)) for k in (1, 3, 2)]


def body(params, momentum, tokens, targets, blend_weight):
    weight = params[0].T
    moment = momentum[0].T
    units = weight.shape[0]
    pieces = jnp.swapaxes(tokens[0], 1, 2)
    wanted = jnp.swapaxes(targets[0], 1, 2)
    me = lax.axis_index("shard")[None]
    replicas = lax.axis_size("rep")
    rows = units // UNITS * LINES

    whole = jax.ShapeDtypeStruct((units, D), jnp.float32)
    half = jax.ShapeDtypeStruct((units, D), jnp.bfloat16)
    lines = jax.ShapeDtypeStruct((rows, LANES), jnp.bfloat16)

    first = pieces[0, :TOP], pieces[0, TOP:]
    second = pieces[1, :TOP], pieces[1, TOP:]
    near, far, sent = gather(first)
    second, _ = lax.optimization_barrier((second, sent))
    near2, far2, _ = gather(second)

    near += other_core(near)
    far += other_core(far)
    grad = call(early_kernel(0), whole, (gate(me), weight, wanted), near, False)
    weight_lines, moment, weight = call(
        late_kernel(0), (lines, whole, half), (me, weight, wanted, grad, moment), far, True
    )
    parts = weight_mean(weight_lines)

    near2 += other_core(near2)
    far2 += other_core(far2)
    grad = call(early_kernel(1), whole, (gate(me), weight, wanted), near2, False)
    moment_lines, moment = call(late_kernel(1), (lines, whole), (me, weight, wanted, grad, moment), far2, True)
    got = lax.all_to_all(moment_lines.reshape(replicas, -1, LANES), "rep", 0, 0)
    means = small(mean_kernel, [got], got.shape)
    mean_moment = lax.all_to_all(means, "rep", 0, 0).reshape(-1, LANES)

    mean_weight = pl.pallas_call(
        spread_kernel,
        out_shape=half,
        in_specs=[SMEM] + [VMEM] * 4,
        out_specs=VMEM,
        scratch_shapes=[pltpu.VMEM((rows, LANES), jnp.bfloat16)],
        compiler_params=pltpu.CompilerParams(vmem_limit_bytes=12 * MIB),
        name="spread",
    )(jnp.stack([lax.axis_index("rep"), lax.axis_index("shard")]), *parts)
    block = pl.BlockSpec((UNITS, D), lambda i: (i, 0))
    averaged, blended = pl.pallas_call(
        last_kernel,
        grid=(units // UNITS,),
        out_shape=(whole, whole),
        in_specs=[pl.BlockSpec((UNITS, 1), lambda i: (i, 0)), VMEM, block, block],
        out_specs=(block, block),
        compiler_params=pltpu.CompilerParams(vmem_limit_bytes=12 * MIB),
        name="last",
    )(blend_weight[:, None], mean_moment, mean_weight, pltpu.with_memory_space_constraint(moment, pltpu.HBM))
    return averaged.T, blended.T[None]


def solution(mesh):
    return jax.shard_map(
        body,
        mesh=mesh,
        in_specs=(
            P("rep", None, "shard"),
            P("rep", None, "shard"),
            P("rep", None, "shard", None),
            P("rep", None, None, "shard"),
            P("shard"),
        ),
        out_specs=(P(None, "shard"), P("rep", None, "shard")),
        check_vma=False,
    )
```

profile of v0, /device:TPU:2, one launch (start us, length us, event | category | flops | bytes accessed | tf_op | source)
XLA Modules:
  0.0 216.7 jit_solution(7295802580652651731)
XLA Ops:
  2.1 6.4 %collective-permute-start.3 = (bf16[800,128]{1,0:T(8,128)(2,1)S(1)}, bf16[800,128]{1,0:T(8,128)(2,1)S(1)}, u32[]{:S(2)}, u32[]{:S(2)}) collective-permute-start(bf16[800,128]{1,0:T(8,128)(2,1)S(1)} %get-tuple-element.22.refs_1_), channel_id=1, source_target_pairs={{0,6},{1,7},{2,0},{3,1},{4,2},{5,3},{6,4},{7,5},{8,14},{9,15},{10,... | collective-permute-start | bytes 614408 | tf_op jit(solution)/shard_map/ppermute | solution.py:176
  12.7 7.5 %collective-permute-done.3.refs_5_ = bf16[800,128]{1,0:T(8,128)(2,1)S(1)} collective-permute-done((bf16[800,128]{1,0:T(8,128)(2,1)S(1)}, bf16[800,128]{1,0:T(8,128)(2,1)S(1)}, u32[]{:S(2)}, u32[]{:S(2)}) %collective-permute-start.3) | collective-permute-done | bytes 204832 | tf_op jit(solution)/shard_map/ppermute | solution.py:176
  20.1 4.7 %collective-permute-start.11 = (bf16[800,128]{1,0:T(8,128)(2,1)S(1)}, bf16[800,128]{1,0:T(8,128)(2,1)}, u32[]{:S(2)}, u32[]{:S(2)}) collective-permute-start(bf16[800,128]{1,0:T(8,128)(2,1)S(1)} %collective-permute-done.3.refs_5_), channel_id=1, source_target_pairs={{0,6},{1,7},{2,0},{3,1},{4,2},{5,3},{6,4},{7,5},{8,14},{9,15},{10,... | collective-permute-start | bytes 614408 | tf_op jit(solution)/shard_map/ppermute | solution.py:176
  24.9 5.6 %collective-permute-done.1.refs_3_ = bf16[800,128]{1,0:T(8,128)(2,1)S(1)} collective-permute-done((bf16[800,128]{1,0:T(8,128)(2,1)S(1)}, bf16[800,128]{1,0:T(8,128)(2,1)S(1)}, u32[]{:S(2)}, u32[]{:S(2)}) %collective-permute-start.1) | collective-permute-done | bytes 204832 | tf_op jit(solution)/shard_map/ppermute | solution.py:176
  31.7 3.7 %collective-permute-done.11.refs_1_ = bf16[800,128]{1,0:T(8,128)(2,1)} collective-permute-done((bf16[800,128]{1,0:T(8,128)(2,1)S(1)}, bf16[800,128]{1,0:T(8,128)(2,1)}, u32[]{:S(2)}, u32[]{:S(2)}) %collective-permute-start.11) | collective-permute-done | bytes 204832 | tf_op jit(solution)/shard_map/ppermute | solution.py:176
  35.4 4.7 %collective-permute-start.16 = (bf16[800,128]{1,0:T(8,128)(2,1)S(1)}, bf16[800,128]{1,0:T(8,128)(2,1)}, u32[]{:S(2)}, u32[]{:S(2)}) collective-permute-start(bf16[800,128]{1,0:T(8,128)(2,1)S(1)} %get-tuple-element.12.refs_0_), channel_id=1, source_target_pairs={{0,6},{1,7},{2,0},{3,1},{4,2},{5,3},{6,4},{7,5},{8,14},{9,15},{10,... | collective-permute-start | bytes 614408 | tf_op jit(solution)/shard_map/ppermute | solution.py:176
  42.1 4.1 %collective-permute-start.17 = (bf16[800,128]{1,0:T(8,128)(2,1)S(1)}, bf16[800,128]{1,0:T(8,128)(2,1)}, u32[]{:S(2)}, u32[]{:S(2)}) collective-permute-start(bf16[800,128]{1,0:T(8,128)(2,1)S(1)} %get-tuple-element.13.refs_1_), channel_id=1, source_target_pairs={{0,6},{1,7},{2,0},{3,1},{4,2},{5,3},{6,4},{7,5},{8,14},{9,15},{10,... | collective-permute-start | bytes 614408 | tf_op jit(solution)/shard_map/ppermute | solution.py:176
  49.5 3.2 %collective-permute-done.14.refs_2_ = bf16[800,128]{1,0:T(8,128)(2,1)} collective-permute-done((bf16[800,128]{1,0:T(8,128)(2,1)S(1)}, bf16[800,128]{1,0:T(8,128)(2,1)}, u32[]{:S(2)}, u32[]{:S(2)}) %collective-permute-start.14) | collective-permute-done | bytes 204832 | tf_op jit(solution)/shard_map/ppermute | solution.py:176
  53.8 4.0 %collective-permute-done.17.refs_5_ = bf16[800,128]{1,0:T(8,128)(2,1)} collective-permute-done((bf16[800,128]{1,0:T(8,128)(2,1)S(1)}, bf16[800,128]{1,0:T(8,128)(2,1)}, u32[]{:S(2)}, u32[]{:S(2)}) %collective-permute-start.17) | collective-permute-done | bytes 204832 | tf_op jit(solution)/shard_map/ppermute | solution.py:176
  60.2 5.8 %collective-permute-done.10.refs_0_ = bf16[800,128]{1,0:T(8,128)(2,1)} collective-permute-done((bf16[800,128]{1,0:T(8,128)(2,1)S(1)}, bf16[800,128]{1,0:T(8,128)(2,1)}, u32[]{:S(2)}, u32[]{:S(2)}) %collective-permute-start.10) | collective-permute-done | bytes 204832 | tf_op jit(solution)/shard_map/ppermute | solution.py:176
  68.6 3.2 %collective-permute-done.24.refs_0_ = bf16[800,128]{1,0:T(8,128)(2,1)} collective-permute-done((bf16[800,128]{1,0:T(8,128)(2,1)}, bf16[800,128]{1,0:T(8,128)(2,1)}, u32[]{:S(2)}, u32[]{:S(2)}) %collective-permute-start.24) | collective-permute-done | bytes 204832 | tf_op jit(solution)/shard_map/ppermute | solution.py:176
  78.3 4.9 %shard_map.69.grad = f32[400,1600]{1,0:T(8,128)S(1)} custom-call(s32[1]{0:T(128)} %shard_map.68.me, f32[400,1600]{1,0:T(8,128)S(1)} %bitcast.34, bf16[2,400,1024]{2,1,0:T(8,128)(2,1)S(1)} %bitcast.30, bf16[800,128]{1,0:T(8,128)(2,1)S(1)} %get-tuple-element.23.refs_0_, bf16[800,128]{1,0:T(8,128)(2,1)S(1)} %get-tuple-element.22.refs_1_, ...), custom_call_target="tpu_custom_call" | custom-call | flops 1966080000 | bytes 5120000 | tf_op jit(solution)/shard_map/pallas_call | solution.py:148
  84.1 5.9 %shard_map.70 = (bf16[5120,128]{1,0:T(8,128)(2,1)}, f32[400,1600]{1,0:T(8,128)}, bf16[400,1600]{1,0:T(8,128)(2,1)}) custom-call(s32[1]{0:T(128)} %bitcast.1.me, f32[400,1600]{1,0:T(8,128)S(1)} %bitcast.35, bf16[2,400,1024]{2,1,0:T(8,128)(2,1)S(1)} %bitcast.31, f32[400,1600]{1,0:T(8,128)S(1)} %shard_map.69.grad, f32[400,1600]{1,0:T(8,128)S(1)} %bitcast.37, ...), custom_call_target="tpu_custom_call" | custom-call | flops 655360000 | bytes 5120000 | tf_op jit(solution)/shard_map/pallas_call | solution.py:148
  91.4 6.2 %shard_map.71.grad = f32[400,1600]{1,0:T(8,128)S(1)} custom-call(s32[1]{0:T(128)} %shard_map.68.me, bf16[400,1600]{1,0:T(8,128)(2,1)S(1)} %copy-done.2, bf16[2,400,1024]{2,1,0:T(8,128)(2,1)S(1)} %bitcast.32, bf16[800,128]{1,0:T(8,128)(2,1)S(1)} %get-tuple-element.12.refs_0_, bf16[800,128]{1,0:T(8,128)(2,1)S(1)} %get-tuple-element.13.refs_1_, ...), custom_call_target="tpu_custom_call" | custom-call | flops 1966080000 | bytes 5120000 | tf_op jit(solution)/shard_map/pallas_call | solution.py:148
  97.6 5.0 %shard_map.72 = (bf16[5120,128]{1,0:T(8,128)(2,1)}, f32[400,1600]{1,0:T(8,128)}) custom-call(s32[1]{0:T(128)} %bitcast.1.me, bf16[400,1600]{1,0:T(8,128)(2,1)S(1)} %copy-done.2, bf16[2,400,1024]{2,1,0:T(8,128)(2,1)S(1)} %bitcast.33, f32[400,1600]{1,0:T(8,128)S(1)} %shard_map.71.grad, f32[400,1600]{1,0:T(8,128)S(1)} %copy-done.4, ...), custom_call_target="tpu_custom_call" | custom-call | flops 655360000 | bytes 5120000 | tf_op jit(solution)/shard_map/pallas_call | solution.py:148
  102.6 34.5 %all_to_all.15.got = bf16[32,160,128]{2,1,0:T(8,128)(2,1)S(1)} all-to-all(bf16[32,160,128]{2,1,0:T(8,128)(2,1)} %bitcast.39), channel_id=1, replica_groups=mesh['rep'=32,'shard'=8] {'rep'}, dimensions={0} | all-to-all | bytes 2621440 | tf_op jit(solution)/shard_map/all_to_all | solution.py:284
  137.1 4.9 %all-to-all-start.2 = ((bf16[16,320,128]{2,1,0:T(8,128)(2,1)}), bf16[16,320,128]{2,1,0:T(8,128)(2,1)S(1)}, u32[]{:S(2)}, u32[]{:S(2)}) async-start(bf16[16,320,128]{2,1,0:T(8,128)(2,1)} %bitcast.38), calls=%async_computation.2 | async-start | bytes 2621440 | tf_op jit(solution)/shard_map/all_to_all | solution.py:242
  143.3 15.8 %all-to-all-done.2.got = bf16[16,320,128]{2,1,0:T(8,128)(2,1)S(1)} async-done(((bf16[16,320,128]{2,1,0:T(8,128)(2,1)}), bf16[16,320,128]{2,1,0:T(8,128)(2,1)S(1)}, u32[]{:S(2)}, u32[]{:S(2)}) %all-to-all-start.2) | async-done | bytes 1310752 | tf_op jit(solution)/shard_map/all_to_all | solution.py:242
  159.1 6.4 %all-to-all-start.1 = ((bf16[32,160,128]{2,1,0:T(8,128)(2,1)}), bf16[32,160,128]{2,1,0:T(8,128)(2,1)S(1)}, u32[]{:S(2)}, u32[]{:S(2)}) async-start(bf16[32,160,128]{2,1,0:T(8,128)(2,1)} %shard_map.73), calls=%async_computation.1 | async-start | bytes 2621440 | tf_op jit(solution)/shard_map/all_to_all | solution.py:286
  167.3 14.2 %collective-permute-done.28.there = bf16[320,128]{1,0:T(8,128)(2,1)S(1)} collective-permute-done((bf16[320,128]{1,0:T(8,128)(2,1)S(1)}, bf16[320,128]{1,0:T(8,128)(2,1)S(1)}, u32[]{:S(2)}, u32[]{:S(2)}) %collective-permute-start.28) | collective-permute-done | bytes 81952 | tf_op jit(solution)/shard_map/ppermute | solution.py:237
  188.9 5.8 %collective-permute-done.29.refs_1_ = bf16[320,128]{1,0:T(8,128)(2,1)S(1)} collective-permute-done((bf16[320,128]{1,0:T(8,128)(2,1)S(1)}, bf16[320,128]{1,0:T(8,128)(2,1)S(1)}, u32[]{:S(2)}, u32[]{:S(2)}) %collective-permute-start.29) | collective-permute-done | bytes 81952 | tf_op jit(solution)/shard_map/ppermute | solution.py:237
  199.0 4.5 %collective-permute-done.34.refs_3_ = bf16[1280,128]{1,0:T(8,128)(2,1)S(1)} collective-permute-done((bf16[1280,128]{1,0:T(8,128)(2,1)S(1)}, bf16[1280,128]{1,0:T(8,128)(2,1)S(1)}, u32[]{:S(2)}, u32[]{:S(2)}) %collective-permute-start.34) | collective-permute-done | bytes 327712 | tf_op jit(solution)/shard_map/ppermute | solution.py:237
  203.5 3.4 %collective-permute-done.33.refs_2_ = bf16[1280,128]{1,0:T(8,128)(2,1)S(1)} collective-permute-done((bf16[1280,128]{1,0:T(8,128)(2,1)S(1)}, bf16[1280,128]{1,0:T(8,128)(2,1)S(1)}, u32[]{:S(2)}, u32[]{:S(2)}) %collective-permute-start.33) | collective-permute-done | bytes 327712 | tf_op jit(solution)/shard_map/ppermute | solution.py:237
  211.2 5.5 %last.1 = (f32[400,1600]{1,0:T(8,128)}, f32[400,1600]{1,0:T(8,128)}) custom-call(f32[400,1]{1,0:T(8,128)S(1)} %copy.7.blend, bf16[5120,128]{1,0:T(8,128)(2,1)S(1)} %bitcast.36, bf16[400,1600]{1,0:T(8,128)(2,1)S(1)} %spread.1.mean_weight, f32[400,1600]{1,0:T(8,128)} %get-tuple-element.17.moment), custom_call_target="tpu_custom_call" | custom-call | tf_op jit(solution)/shard_map/last/pallas_call | solution.py:298
  (113 shorter events, 46.1 us)
Async XLA Ops:
  2.1 18.0 %collective-permute-start.3 = (bf16[800,128]{1,0:T(8,128)(2,1)S(1)}, bf16[800,128]{1,0:T(8,128)(2,1)S(1)}, u32[]{:S(2)}, u32[]{:S(2)}) collective-permute-start(bf16[800,128]{1,0:T(8,128)(2,1)S(1)} %get-tuple-element.22.refs_1_), channel_id=1, source_target_pairs={{0,6},{1,7},{2,0},{3,1},{4,2},{5,3},{6,4},{7,5},{8,14},{9,15},{10,... | collective-permute-start | bytes 614408 | tf_op jit(solution)/shard_map/ppermute | solution.py:176
  8.5 16.4 %collective-permute-start = (bf16[800,128]{1,0:T(8,128)(2,1)S(1)}, bf16[800,128]{1,0:T(8,128)(2,1)S(1)}, u32[]{:S(2)}, u32[]{:S(2)}) collective-permute-start(bf16[800,128]{1,0:T(8,128)(2,1)S(1)} %get-tuple-element.23.refs_0_), channel_id=1, source_target_pairs={{0,2},{1,3},{2,4},{3,5},{4,6},{5,7},{6,0},{7,1},{8,10},{9,11},{10,... | collective-permute-start | bytes 614408 | tf_op jit(solution)/shard_map/ppermute | solution.py:176
  8.5 22.0 %collective-permute-start.1 = (bf16[800,128]{1,0:T(8,128)(2,1)S(1)}, bf16[800,128]{1,0:T(8,128)(2,1)S(1)}, u32[]{:S(2)}, u32[]{:S(2)}) collective-permute-start(bf16[800,128]{1,0:T(8,128)(2,1)S(1)} %get-tuple-element.22.refs_1_), channel_id=1, source_target_pairs={{0,2},{1,3},{2,4},{3,5},{4,6},{5,7},{6,0},{7,1},{8,10},{9,11},{10,... | collective-permute-start | bytes 614408 | tf_op jit(solution)/shard_map/ppermute | solution.py:176
  10.1 20.4 %collective-permute-start.2 = (bf16[800,128]{1,0:T(8,128)(2,1)S(1)}, bf16[800,128]{1,0:T(8,128)(2,1)S(1)}, u32[]{:S(2)}, u32[]{:S(2)}) collective-permute-start(bf16[800,128]{1,0:T(8,128)(2,1)S(1)} %get-tuple-element.23.refs_0_), channel_id=1, source_target_pairs={{0,6},{1,7},{2,0},{3,1},{4,2},{5,3},{6,4},{7,5},{8,14},{9,15},{10,... | collective-permute-start | bytes 614408 | tf_op jit(solution)/shard_map/ppermute | solution.py:176
  12.7 18.3 %collective-permute-start.4 = (bf16[800,128]{1,0:T(8,128)(2,1)S(1)}, bf16[800,128]{1,0:T(8,128)(2,1)S(1)}, u32[]{:S(2)}, u32[]{:S(2)}) collective-permute-start(bf16[800,128]{1,0:T(8,128)(2,1)S(1)} %get-tuple-element.23.refs_0_), channel_id=1, source_target_pairs={{0,1},{1,0},{2,3},{3,2},{4,5},{5,4},{6,7},{7,6},{8,9},{9,8},{10,11... | collective-permute-start | bytes 614408 | tf_op jit(solution)/shard_map/ppermute | solution.py:176
  20.1 15.3 %collective-permute-start.11 = (bf16[800,128]{1,0:T(8,128)(2,1)S(1)}, bf16[800,128]{1,0:T(8,128)(2,1)}, u32[]{:S(2)}, u32[]{:S(2)}) collective-permute-start(bf16[800,128]{1,0:T(8,128)(2,1)S(1)} %collective-permute-done.3.refs_5_), channel_id=1, source_target_pairs={{0,6},{1,7},{2,0},{3,1},{4,2},{5,3},{6,4},{7,5},{8,14},{9,15},{10,... | collective-permute-start | bytes 614408 | tf_op jit(solution)/shard_map/ppermute | solution.py:176
  24.9 15.2 %collective-permute-start.9 = (bf16[800,128]{1,0:T(8,128)(2,1)S(1)}, bf16[800,128]{1,0:T(8,128)(2,1)S(1)}, u32[]{:S(2)}, u32[]{:S(2)}) collective-permute-start(bf16[800,128]{1,0:T(8,128)(2,1)S(1)} %collective-permute-done.3.refs_5_), channel_id=1, source_target_pairs={{0,1},{1,0},{2,3},{3,2},{4,5},{5,4},{6,7},{7,6},{8,9},{9,8},{10,11... | collective-permute-start | bytes 614408 | tf_op jit(solution)/shard_map/ppermute | solution.py:176
  31.7 14.6 %collective-permute-start.18 = (bf16[800,128]{1,0:T(8,128)(2,1)S(1)}, bf16[800,128]{1,0:T(8,128)(2,1)S(1)}, u32[]{:S(2)}, u32[]{:S(2)}) collective-permute-start(bf16[800,128]{1,0:T(8,128)(2,1)S(1)} %get-tuple-element.12.refs_0_), channel_id=1, source_target_pairs={{0,1},{1,0},{2,3},{3,2},{4,5},{5,4},{6,7},{7,6},{8,9},{9,8},{10,11... | collective-permute-start | bytes 614408 | tf_op jit(solution)/shard_map/ppermute | solution.py:176
  40.8 11.9 %collective-permute-start.14 = (bf16[800,128]{1,0:T(8,128)(2,1)S(1)}, bf16[800,128]{1,0:T(8,128)(2,1)}, u32[]{:S(2)}, u32[]{:S(2)}) collective-permute-start(bf16[800,128]{1,0:T(8,128)(2,1)S(1)} %get-tuple-element.12.refs_0_), channel_id=1, source_target_pairs={{0,2},{1,3},{2,4},{3,5},{4,6},{5,7},{6,0},{7,1},{8,10},{9,11},{10,... | collective-permute-start | bytes 614408 | tf_op jit(solution)/shard_map/ppermute | solution.py:176
  42.1 15.6 %collective-permute-start.17 = (bf16[800,128]{1,0:T(8,128)(2,1)S(1)}, bf16[800,128]{1,0:T(8,128)(2,1)}, u32[]{:S(2)}, u32[]{:S(2)}) collective-permute-start(bf16[800,128]{1,0:T(8,128)(2,1)S(1)} %get-tuple-element.13.refs_1_), channel_id=1, source_target_pairs={{0,6},{1,7},{2,0},{3,1},{4,2},{5,3},{6,4},{7,5},{8,14},{9,15},{10,... | collective-permute-start | bytes 614408 | tf_op jit(solution)/shard_map/ppermute | solution.py:176
  47.0 19.0 %collective-permute-start.10 = (bf16[800,128]{1,0:T(8,128)(2,1)S(1)}, bf16[800,128]{1,0:T(8,128)(2,1)}, u32[]{:S(2)}, u32[]{:S(2)}) collective-permute-start(bf16[800,128]{1,0:T(8,128)(2,1)S(1)} %collective-permute-done.refs_2_), channel_id=1, source_target_pairs={{0,2},{1,3},{2,4},{3,5},{4,6},{5,7},{6,0},{7,1},{8,10},{9,11},{10,... | collective-permute-start | bytes 614408 | tf_op jit(solution)/shard_map/ppermute | solution.py:176
  52.6 14.1 %collective-permute-start.6 = (bf16[800,128]{1,0:T(8,128)(2,1)S(1)}, bf16[800,128]{1,0:T(8,128)(2,1)S(1)}, u32[]{:S(2)}, u32[]{:S(2)}) collective-permute-start(bf16[800,128]{1,0:T(8,128)(2,1)S(1)} %collective-permute-done.refs_2_), channel_id=1, source_target_pairs={{0,1},{1,0},{2,3},{3,2},{4,5},{5,4},{6,7},{7,6},{8,9},{9,8},{10,11... | collective-permute-start | bytes 614408 | tf_op jit(solution)/shard_map/ppermute | solution.py:176
  53.3 14.6 %collective-permute-start.13 = (bf16[800,128]{1,0:T(8,128)(2,1)}, bf16[800,128]{1,0:T(8,128)(2,1)}, u32[]{:S(2)}, u32[]{:S(2)}) collective-permute-start(bf16[800,128]{1,0:T(8,128)(2,1)} %collective-permute-done.11.refs_1_), channel_id=1, source_target_pairs={{0,1},{1,0},{2,3},{3,2},{4,5},{5,4},{6,7},{7,6},{8,9},{9,8},{10,11... | collective-permute-start | bytes 614408 | tf_op jit(solution)/shard_map/ppermute | solution.py:176
  58.7 13.2 %collective-permute-start.24 = (bf16[800,128]{1,0:T(8,128)(2,1)}, bf16[800,128]{1,0:T(8,128)(2,1)}, u32[]{:S(2)}, u32[]{:S(2)}) collective-permute-start(bf16[800,128]{1,0:T(8,128)(2,1)} %collective-permute-done.14.refs_2_), channel_id=1, source_target_pairs={{0,2},{1,3},{2,4},{3,5},{4,6},{5,7},{6,0},{7,1},{8,10},{9,11},{10,... | collective-permute-start | bytes 614408 | tf_op jit(solution)/shard_map/ppermute | solution.py:176
  66.0 17.1 %collective-permute-start.25 = (bf16[800,128]{1,0:T(8,128)(2,1)}, bf16[800,128]{1,0:T(8,128)(2,1)}, u32[]{:S(2)}, u32[]{:S(2)}) collective-permute-start(bf16[800,128]{1,0:T(8,128)(2,1)} %collective-permute-done.17.refs_5_), channel_id=1, source_target_pairs={{0,6},{1,7},{2,0},{3,1},{4,2},{5,3},{6,4},{7,5},{8,14},{9,15},{10,... | collective-permute-start | bytes 614408 | tf_op jit(solution)/shard_map/ppermute | solution.py:176
  67.4 16.4 %collective-permute-start.12 = (bf16[800,128]{1,0:T(8,128)(2,1)}, bf16[800,128]{1,0:T(8,128)(2,1)}, u32[]{:S(2)}, u32[]{:S(2)}) collective-permute-start(bf16[800,128]{1,0:T(8,128)(2,1)} %collective-permute-done.10.refs_0_), channel_id=1, source_target_pairs={{0,1},{1,0},{2,3},{3,2},{4,5},{5,4},{6,7},{7,6},{8,9},{9,8},{10,11... | collective-permute-start | bytes 614408 | tf_op jit(solution)/shard_map/ppermute | solution.py:176
  67.9 22.1 %collective-permute-start.20 = (bf16[800,128]{1,0:T(8,128)(2,1)}, bf16[800,128]{1,0:T(8,128)(2,1)S(1)}, u32[]{:S(2)}, u32[]{:S(2)}) collective-permute-start(bf16[800,128]{1,0:T(8,128)(2,1)} %collective-permute-done.14.refs_2_), channel_id=1, source_target_pairs={{0,1},{1,0},{2,3},{3,2},{4,5},{5,4},{6,7},{7,6},{8,9},{9,8},{10,11... | collective-permute-start | bytes 614408 | tf_op jit(solution)/shard_map/ppermute | solution.py:176
  68.5 21.5 %collective-permute-start.23 = (bf16[800,128]{1,0:T(8,128)(2,1)}, bf16[800,128]{1,0:T(8,128)(2,1)S(1)}, u32[]{:S(2)}, u32[]{:S(2)}) collective-permute-start(bf16[800,128]{1,0:T(8,128)(2,1)} %collective-permute-done.17.refs_5_), channel_id=1, source_target_pairs={{0,1},{1,0},{2,3},{3,2},{4,5},{5,4},{6,7},{7,6},{8,9},{9,8},{10,11... | collective-permute-start | bytes 614408 | tf_op jit(solution)/shard_map/ppermute | solution.py:176
  71.8 18.2 %collective-permute-start.21 = (bf16[800,128]{1,0:T(8,128)(2,1)}, bf16[800,128]{1,0:T(8,128)(2,1)S(1)}, u32[]{:S(2)}, u32[]{:S(2)}) collective-permute-start(bf16[800,128]{1,0:T(8,128)(2,1)} %collective-permute-done.15.refs_3_), channel_id=1, source_target_pairs={{0,1},{1,0},{2,3},{3,2},{4,5},{5,4},{6,7},{7,6},{8,9},{9,8},{10,11... | collective-permute-start | bytes 614408 | tf_op jit(solution)/shard_map/ppermute | solution.py:176
  83.1 14.4 %collective-permute-start.26 = (bf16[800,128]{1,0:T(8,128)(2,1)}, bf16[800,128]{1,0:T(8,128)(2,1)S(1)}, u32[]{:S(2)}, u32[]{:S(2)}) collective-permute-start(bf16[800,128]{1,0:T(8,128)(2,1)} %collective-permute-done.24.refs_0_), channel_id=1, source_target_pairs={{0,1},{1,0},{2,3},{3,2},{4,5},{5,4},{6,7},{7,6},{8,9},{9,8},{10,11... | collective-permute-start | bytes 614408 | tf_op jit(solution)/shard_map/ppermute | solution.py:176
  83.7 13.8 %collective-permute-start.27 = (bf16[800,128]{1,0:T(8,128)(2,1)}, bf16[800,128]{1,0:T(8,128)(2,1)S(1)}, u32[]{:S(2)}, u32[]{:S(2)}) collective-permute-start(bf16[800,128]{1,0:T(8,128)(2,1)} %collective-permute-done.25.refs_1_), channel_id=1, source_target_pairs={{0,1},{1,0},{2,3},{3,2},{4,5},{5,4},{6,7},{7,6},{8,9},{9,8},{10,11... | collective-permute-start | bytes 614408 | tf_op jit(solution)/shard_map/ppermute | solution.py:176
  137.1 22.0 %all-to-all-start.2 = ((bf16[16,320,128]{2,1,0:T(8,128)(2,1)}), bf16[16,320,128]{2,1,0:T(8,128)(2,1)S(1)}, u32[]{:S(2)}, u32[]{:S(2)}) async-start(bf16[16,320,128]{2,1,0:T(8,128)(2,1)} %bitcast.38), calls=%async_computation.2 | async-start | bytes 2621440 | tf_op jit(solution)/shard_map/all_to_all | solution.py:242
  159.1 52.2 %all-to-all-start.1 = ((bf16[32,160,128]{2,1,0:T(8,128)(2,1)}), bf16[32,160,128]{2,1,0:T(8,128)(2,1)S(1)}, u32[]{:S(2)}, u32[]{:S(2)}) async-start(bf16[32,160,128]{2,1,0:T(8,128)(2,1)} %shard_map.73), calls=%async_computation.1 | async-start | bytes 2621440 | tf_op jit(solution)/shard_map/all_to_all | solution.py:286
  165.7 15.8 %collective-permute-start.28 = (bf16[320,128]{1,0:T(8,128)(2,1)S(1)}, bf16[320,128]{1,0:T(8,128)(2,1)S(1)}, u32[]{:S(2)}, u32[]{:S(2)}) collective-permute-start(bf16[320,128]{1,0:T(8,128)(2,1)S(1)} %shard_map.74.here), channel_id=1, source_target_pairs={{0,32},{1,33},{2,34},{3,35},{4,36},{5,37},{6,38},{7,39},{8,40},{9,... | collective-permute-start | bytes 245768 | tf_op jit(solution)/shard_map/ppermute | solution.py:237
  (37 other events, 269.4 us)
where the time goes:
time: 218 us; the launch traced here: 217 us
  waiting for transfers between devices  79.9 us (37%)
  starting transfers between devices  53.6 us (25%)
  blocking collectives  34.5 us (16%)
  Pallas kernels  30.3 us (14%)
  local copies, waits for them, and re-layouts  17.4 us (8%)
    all_to_all x1, blocking collectives, body(): got = lax.all_to_all(moment_lines.reshape(replicas, -1, LANES), 'rep', 0, 0)  34.5 us
    ppermute x28, waiting for transfers between devices, shard_permute(): return lax.ppermute(v, 'shard', rotated(up, cores))  33.8 us
    ppermute x28, starting transfers between devices, shard_permute(): return lax.ppermute(v, 'shard', rotated(up, cores))  31.6 us
    ppermute x7, waiting for transfers between devices, replica_permute(): return lax.ppermute(v, ('rep', 'shard'), pairs)  30.3 us
    pallas_call x4, Pallas kernels, call(): pl.pallas_call(kernel, out_shape=tuple((pltpu.HBM(o.shape, o.dtype) for o...  22 us
    unnamed x48, local copies, waits for them, and re-layouts  15.9 us
    all_to_all x1, waiting for transfers between devices, weight_mean(): lax.all_to_all(lines.reshape(16, -1, LANES), 'rep', 0, 0, axis_index_grou...  15.8 us
    ppermute x7, starting transfers between devices, replica_permute(): return lax.ppermute(v, ('rep', 'shard'), pairs)  10.7 us
  transfers between devices with their start and end apart: 37, of which 15 were waited for; matrix products, arithmetic and copies ran while one was open for 0% of the time, Pallas kernels for 9%

commit v1 on v0

--- a/solution.py
+++ b/solution.py
@@ -31,32 +31,7 @@
 
 def places(me, ups):
     z, c = me // 2, me % 2
-    return [2 * ((z + up) % 4) + (c + k) % 2 for k in range(2) for up in ups]
-
-
-def partial_gradient(step, at, weight, wanted, blocks, x):
-    for i, (top, bottom) in enumerate(blocks):
-        x[:TOP, i * LANES : (i + 1) * LANES] = top[...]
-        x[TOP:, i * LANES : (i + 1) * LANES] = bottom[...]
-    pre = jnp.dot(weight, x[...], preferred_element_type=jnp.float32) * SCALE
-    want = jnp.concatenate(
-        [wanted[step, :, pl.ds(pl.multiple_of(a * LANES, LANES), LANES)] for a in at], axis=1
-    )
-    hidden = slope(pre, want.astype(jnp.float32)).astype(jnp.bfloat16)
-    return lax.dot_general(hidden, x[...], (((1,), (1,)), ((), ())), preferred_element_type=jnp.float32)
-
-
-def pairs(refs):
-    return [(refs[i], refs[i + 1]) for i in range(0, len(refs), 2)]
-
-
-def early_kernel(step):
-    def kernel(me, weight, wanted, *refs):
-        *blocks, out, x = refs
-        at = places(me[0], (0, 3, 1))
-        out[...] = partial_gradient(step, at, weight[...].astype(jnp.bfloat16), wanted, pairs(blocks), x)
-
-    return kernel
+    return [2 * ((z + up) % 4) + (c + k) % 2 for up in ups for k in range(2)]
 
 
 UNITS = 80
@@ -83,25 +58,76 @@
     yield slice(FULL * LANES, D), jnp.concatenate([rest[:, :half], rest[:, half:]], axis=0)
 
 
-def late_kernel(step):
-    def kernel(me, weight, wanted, grad, moment, *refs):
-        count = 3 if step == 0 else 2
-        blocks, refs = refs[:4], refs[4:]
-        outs, bufs, (x, g, done) = refs[:count], refs[count : 2 * count], refs[2 * count :]
-        at = places(me[0], (2,))
-        g[...] = partial_gradient(step, at, weight[...].astype(jnp.bfloat16), wanted, pairs(blocks), x)
+def step_kernel(step, ups, late):
+    first = step == 0
+
+    def kernel(me, wanted, *refs):
+        extra = 4 if first and late else 1
+        refs, (x, g, m_buf, want, fetched, loaded, stored, *bufs) = refs[: -7 - extra], refs[-7 - extra :]
+        if first and late:
+            full, half, moment, *refs = refs
+        elif first:
+            full, moment, *refs = refs
+        else:
+            half, moment, *refs = refs
+        count = 2 * len(ups) * (1 if step and not late else 2)
+        blocks, outs = refs[:count], refs[count:]
+        units = wanted.shape[1]
+        lines, w_buf, w_half, m_half = bufs if len(bufs) == 4 else (bufs[0], bufs[0], None, None)
+        loads = []
+        if first:
+            loads.append(pltpu.make_async_copy(full, w_buf, loaded.at[0]))
+        if not (first and late):
+            loads.append(pltpu.make_async_copy(moment, m_buf, loaded.at[1]))
+        fetches = []
+        for i, a in enumerate(places(me[0], ups)):
+            lanes = slice(i * LANES, (i + 1) * LANES)
+            theirs = wanted.at[step, :, pl.ds(pl.multiple_of(a * LANES, LANES), LANES)]
+            moves = [(theirs, want.at[:, lanes])]
+            if count == 2 * len(ups):
+                moves.append((blocks[i], x.at[:, lanes]))
+            else:
+                moves += [(blocks[2 * i], x.at[:TOP, lanes]), (blocks[2 * i + 1], x.at[TOP:, lanes])]
+            for k, (part, whole) in enumerate(moves):
+                fetches.append(pltpu.make_async_copy(part, whole, fetched.at[i, k]))
+        if first and not late:
+            loads[0].start()
+        for fetch in fetches:
+            fetch.start()
+        for load in loads[first and not late :]:
+            load.start()
+        for fetch in fetches:
+            fetch.wait()
+        if first and not late:
+            loads[0].wait()
+            half = outs[1]
+            half[...] = w_buf[...].astype(jnp.bfloat16)
+        pre = jnp.dot(half[...], x[...], preferred_element_type=jnp.float32) * SCALE
+        hidden = slope(pre, want[...].astype(jnp.float32)).astype(jnp.bfloat16)
+        g[...] = lax.dot_general(hidden, x[...], (((1,), (1,)), ((), ())), preferred_element_type=jnp.float32)
+        for load in loads[first and not late :]:
+            load.wait()
         copies = []
-        for i in range(weight.shape[0] // UNITS):
-            rows = slice(i * UNITS, (i + 1) * UNITS)
-            taken = [slice(i * LINES, (i + 1) * LINES), rows, rows][:count]
-            m = DECAY * moment[rows, :] + (grad[rows, :] + g[rows, :])
-            bufs[1][rows, :] = m
-            if step == 0:
-                m = weight[rows, :] - LEARN * m
-                bufs[2][rows, :] = m.astype(jnp.bfloat16)
-            pack(bufs[0].at[taken[0], :], m)
-            for k in range(count):
-                copy = pltpu.make_async_copy(bufs[k].at[taken[k], :], outs[k].at[taken[k], :], done.at[k, i])
+        for i in range(units // UNITS):
+            rows, span = slice(i * UNITS, (i + 1) * UNITS), slice(i * LINES, (i + 1) * LINES)
+            if first and late:
+                m = moment[rows, :] + g[rows, :]
+                w = w_buf[rows, :] - LEARN * m
+                w_half[rows, :] = w.astype(jnp.bfloat16)
+                m_half[rows, :] = m.astype(jnp.bfloat16)
+                pack(lines.at[span, :], w)
+                moves = [(lines, span), (w_half, rows), (m_half, rows)]
+            elif first:
+                outs[0][rows, :] = DECAY * m_buf[rows, :] + g[rows, :]
+                moves = []
+            elif late:
+                pack(lines.at[span, :], m_buf[rows, :] + g[rows, :])
+                moves = [(lines, span)]
+            else:
+                g[rows, :] = DECAY * m_buf[rows, :].astype(jnp.float32) + g[rows, :]
+                moves = [(g, rows)]
+            for o, (buf, part) in enumerate(moves):
+                copy = pltpu.make_async_copy(buf.at[part, :], outs[o].at[part, :], stored.at[o, i])
                 copy.start()
                 copies.append(copy)
         for copy in copies:
@@ -110,11 +136,32 @@
     return kernel
 
 
-def last_kernel(blend, lines, mean_weight, moment, averaged, blended):
-    b = blend[...]
-    for lanes, m in unpacked(lines, pl.multiple_of(pl.program_id(0) * LINES, LINES)):
-        averaged[:, lanes] = mean_weight[:, lanes].astype(jnp.float32) - LEARN * m
-        blended[:, lanes] = b * m + (1.0 - b) * moment[:, lanes]
+def last_kernel(blend, lines, mean_weight, moment, averaged, blended, m_buf, w_buf, a_buf, b_buf, loaded, stored):
+    loads, copies = [], []
+    count = averaged.shape[0] // UNITS
+    parts = [(slice(i * UNITS, (i + 1) * UNITS), slice(i * LINES, (i + 1) * LINES)) for i in range(count)]
+    for i, (rows, span) in enumerate(parts):
+        loads.append(
+            [
+                pltpu.make_async_copy(mean_weight.at[rows, :], w_buf.at[rows, :], loaded.at[0, i]),
+                pltpu.make_async_copy(moment.at[span, :], m_buf.at[span, :], loaded.at[1, i]),
+            ]
+        )
+        for load in loads[-1]:
+            load.start()
+    for i, (rows, span) in enumerate(parts):
+        for load in loads[i]:
+            load.wait()
+        b = blend[rows, :]
+        for (lanes, m), (_, own) in zip(unpacked(lines, i * LINES), unpacked(m_buf, i * LINES)):
+            a_buf[rows, lanes] = w_buf[rows, lanes].astype(jnp.float32) - LEARN * m
+            b_buf[rows, lanes] = b * m + (1.0 - b) * own
+        for k, (buf, out) in enumerate([(a_buf, averaged), (b_buf, blended)]):
+            copy = pltpu.make_async_copy(buf.at[rows, :], out.at[rows, :], stored.at[k, i])
+            copy.start()
+            copies.append(copy)
+    for copy in copies:
+        copy.wait()
 
 
 ROUND = (0, 3, 1, 2)
@@ -139,23 +186,47 @@
 MIB = 1 << 20
 
 
-def call(kernel, outs, args, blocks, late):
-    tokens, units = LANES * len(blocks) // 2, args[1].shape[0]
-    scratch = [pltpu.VMEM((D, tokens), jnp.bfloat16)]
-    if late:
-        scratch = [pltpu.VMEM(o.shape, o.dtype) for o in outs] + scratch + [pltpu.VMEM((units, D), jnp.float32)]
-        scratch.append(pltpu.SemaphoreType.DMA((len(outs), units // UNITS)))
+FAR = pl.BlockSpec(memory_space=pltpu.HBM)
+
+
+def kept(v):
+    return pltpu.with_memory_space_constraint(v, pltpu.HBM)
+
+
+def local_step(me, wanted, weights, moment, blocks, step, ups):
+    first, late = step == 0, ups == (2,)
+    units, tokens = wanted.shape[1], 2 * LANES * len(ups)
+    whole, half = ((units, D), jnp.float32), ((units, D), jnp.bfloat16)
+    lines = (units // UNITS * LINES, LANES), jnp.bfloat16
+    outs = [[[whole], [lines]], [[whole, half], [lines, half, half]]][first][late]
+    bufs = [lines if late else whole if first else ((8, LANES), jnp.bfloat16)]
+    if first and late:
+        bufs = [lines, whole, half, half]
+    here = first and not late
+    args = [kept(w) if w.dtype == jnp.float32 else w for w in weights]
+    specs = [FAR if w.dtype == jnp.float32 else VMEM for w in weights]
+    args.append(moment if first and late else kept(moment))
+    specs.append(VMEM if first and late else FAR)
     return pl.pallas_call(
-        kernel,
-        out_shape=tuple(pltpu.HBM(o.shape, o.dtype) for o in outs) if late else outs,
-        in_specs=[SMEM] + [VMEM] * (len(args) - 1 + len(blocks)),
-        out_specs=(pl.BlockSpec(memory_space=pltpu.HBM),) * len(outs) if late else VMEM,
-        scratch_shapes=scratch,
+        step_kernel(step, ups, late),
+        out_shape=tuple(jax.ShapeDtypeStruct(*o) if here else pltpu.HBM(*o) for o in outs),
+        in_specs=[SMEM, FAR, *specs] + [pl.BlockSpec(memory_space=pl.ANY)] * len(blocks),
+        out_specs=(VMEM if here else FAR,) * len(outs),
+        scratch_shapes=[
+            pltpu.VMEM((D, tokens), jnp.bfloat16),
+            pltpu.VMEM(*whole),
+            pltpu.VMEM(moment.shape, moment.dtype),
+            pltpu.VMEM((units, tokens), jnp.bfloat16),
+            pltpu.SemaphoreType.DMA((2 * len(ups), 3)),
+            pltpu.SemaphoreType.DMA((2,)),
+            pltpu.SemaphoreType.DMA((len(outs), units // UNITS)),
+            *[pltpu.VMEM(*b) for b in bufs],
+        ],
         cost_estimate=pl.CostEstimate(
             flops=4 * tokens * units * D, bytes_accessed=8 * units * D, transcendentals=tokens * units
         ),
         compiler_params=pltpu.CompilerParams(vmem_limit_bytes=24 * MIB),
-    )(*args, *blocks)
+    )(me, kept(wanted), *args, *blocks)
 
 
 def gate_kernel(me, out):
@@ -177,19 +248,30 @@
 
 
 def gather(piece):
-    top, bottom = piece
+    top, bottom = piece[:TOP], piece[TOP:]
     low_top = shard_permute(top, 1, 0)
     high_bottom = shard_permute(bottom, -1, 0)
     low_bottom = shard_permute(bottom, 1, 0)
     high_top = shard_permute(top, -1, 0)
-    far_top = shard_permute(low_top, 1, 0)
-    far_bottom = shard_permute(high_bottom, -1, 0)
-    near = [top, bottom, low_top, low_bottom, high_top, high_bottom]
-    return near, [far_top, far_bottom], (low_top, high_bottom)
-
-
-def other_core(values):
-    return [shard_permute(v, 0, 1) for v in values]
+    far = [shard_permute(low_top, 1, 0), shard_permute(high_bottom, -1, 0)]
+    return both_cores([top, bottom, low_top, low_bottom, high_top, high_bottom]), both_cores(far), (low_bottom, high_top)
+
+
+def gather_whole(piece):
+    low, high = shard_permute(piece, 1, 0), shard_permute(piece, -1, 0)
+    far = [shard_permute(low[:TOP], 1, 0), shard_permute(high[TOP:], -1, 0)]
+    near = []
+    for v in (piece, low, high):
+        near += [v, shard_permute(v, 0, 1)]
+    return near, both_cores(far)
+
+
+def both_cores(values):
+    swapped = [shard_permute(v, 0, 1) for v in values]
+    out = []
+    for i in range(0, len(values), 2):
+        out += values[i : i + 2] + swapped[i : i + 2]
+    return out
 
 
 def added(got):
@@ -261,49 +343,47 @@
 
     whole = jax.ShapeDtypeStruct((units, D), jnp.float32)
     half = jax.ShapeDtypeStruct((units, D), jnp.bfloat16)
-    lines = jax.ShapeDtypeStruct((rows, LANES), jnp.bfloat16)
-
-    first = pieces[0, :TOP], pieces[0, TOP:]
-    second = pieces[1, :TOP], pieces[1, TOP:]
-    near, far, sent = gather(first)
-    second, _ = lax.optimization_barrier((second, sent))
-    near2, far2, _ = gather(second)
-
-    near += other_core(near)
-    far += other_core(far)
-    grad = call(early_kernel(0), whole, (gate(me), weight, wanted), near, False)
-    weight_lines, moment, weight = call(
-        late_kernel(0), (lines, whole, half), (me, weight, wanted, grad, moment), far, True
-    )
+
+    near, far, sent = gather(pieces[0])
+    second, _ = lax.optimization_barrier((pieces[1], sent))
+    near2, far2 = gather_whole(second)
+
+    ready = gate(me)
+    moment, old = local_step(ready, wanted, [weight], moment, near, 0, (0, 3, 1))
+    weight_lines, weight, moment = local_step(me, wanted, [weight, old], moment, far, 0, (2,))
     parts = weight_mean(weight_lines)
 
-    near2 += other_core(near2)
-    far2 += other_core(far2)
-    grad = call(early_kernel(1), whole, (gate(me), weight, wanted), near2, False)
-    moment_lines, moment = call(late_kernel(1), (lines, whole), (me, weight, wanted, grad, moment), far2, True)
+    (moment,) = local_step(me, wanted, [weight], moment, near2, 1, (0, 3, 1))
+    (moment_lines,) = local_step(me, wanted, [weight], moment, far2, 1, (2,))
     got = lax.all_to_all(moment_lines.reshape(replicas, -1, LANES), "rep", 0, 0)
     means = small(mean_kernel, [got], got.shape)
     mean_moment = lax.all_to_all(means, "rep", 0, 0).reshape(-1, LANES)
 
     mean_weight = pl.pallas_call(
         spread_kernel,
-        out_shape=half,
+        out_shape=pltpu.HBM(half.shape, half.dtype),
         in_specs=[SMEM] + [VMEM] * 4,
         out_specs=VMEM,
         scratch_shapes=[pltpu.VMEM((rows, LANES), jnp.bfloat16)],
         compiler_params=pltpu.CompilerParams(vmem_limit_bytes=12 * MIB),
         name="spread",
     )(jnp.stack([lax.axis_index("rep"), lax.axis_index("shard")]), *parts)
-    block = pl.BlockSpec((UNITS, D), lambda i: (i, 0))
     averaged, blended = pl.pallas_call(
         last_kernel,
-        grid=(units // UNITS,),
         out_shape=(whole, whole),
-        in_specs=[pl.BlockSpec((UNITS, 1), lambda i: (i, 0)), VMEM, block, block],
-        out_specs=(block, block),
-        compiler_params=pltpu.CompilerParams(vmem_limit_bytes=12 * MIB),
+        in_specs=[VMEM, VMEM, FAR, FAR],
+        out_specs=(FAR, FAR),
+        scratch_shapes=[
+            pltpu.VMEM((rows, LANES), jnp.bfloat16),
+            pltpu.VMEM((units, D), jnp.bfloat16),
+            pltpu.VMEM((units, D), jnp.float32),
+            pltpu.VMEM((units, D), jnp.float32),
+            pltpu.SemaphoreType.DMA((2, units // UNITS)),
+            pltpu.SemaphoreType.DMA((2, units // UNITS)),
+        ],
+        compiler_params=pltpu.CompilerParams(vmem_limit_bytes=16 * MIB),
         name="last",
-    )(blend_weight[:, None], mean_moment, mean_weight, pltpu.with_memory_space_constraint(moment, pltpu.HBM))
+    )(blend_weight[:, None], mean_moment, kept(mean_weight), kept(moment_lines))
     return averaged.T, blended.T[None]
 
 

time: 218 us -> 206 us (0.945)
  the two profiles are of different devices: /device:TPU:2 before, /device:TPU:8 now
where the time goes in v1:
time: 206 us; the launch traced here: 204 us
  waiting for transfers between devices  79.8 us (39%)
  starting transfers between devices  45.1 us (22%)
  Pallas kernels  31.1 us (15%)
  blocking collectives  27.5 us (13%)
  local copies, waits for them, and re-layouts  19 us (9%)
    ppermute x23, waiting for transfers between devices, shard_permute(): return lax.ppermute(v, 'shard', rotated(up, cores))  37.7 us
    all_to_all x1, blocking collectives, body(): got = lax.all_to_all(moment_lines.reshape(replicas, -1, LANES), 'rep', 0, 0)  27.5 us
    ppermute x7, waiting for transfers between devices, replica_permute(): return lax.ppermute(v, ('rep', 'shard'), pairs)  25.3 us
    ppermute x23, starting transfers between devices, shard_permute(): return lax.ppermute(v, 'shard', rotated(up, cores))  23.4 us
    pallas_call x4, Pallas kernels, local_step(): pl.pallas_call(step_kernel(step, ups, late), out_shape=tuple((jax.ShapeDt...  23.4 us
    all_to_all x1, waiting for transfers between devices, weight_mean(): lax.all_to_all(lines.reshape(16, -1, LANES), 'rep', 0, 0, axis_index_grou...  16.8 us
    unnamed x48, local copies, waits for them, and re-layouts  15.4 us
    ppermute x7, starting transfers between devices, replica_permute(): return lax.ppermute(v, ('rep', 'shard'), pairs)  11.2 us
  transfers between devices with their start and end apart: 32, of which 14 were waited for; matrix products, arithmetic and copies ran while one was open for 1% of the time, Pallas kernels for 11%

profile of v1, /device:TPU:8, one launch (start us, length us, event | category | flops | bytes accessed | tf_op | source)
XLA Modules:
  0.0 203.6 jit_solution(11123945996953581732)
XLA Ops:
  1.7 3.3 %collective-permute-start.2 = (bf16[800,128]{1,0:T(8,128)(2,1)S(1)}, bf16[800,128]{1,0:T(8,128)(2,1)S(1)}, u32[]{:S(2)}, u32[]{:S(2)}) collective-permute-start(bf16[800,128]{1,0:T(8,128)(2,1)S(1)} %get-tuple-element.19.refs_2_), channel_id=1, source_target_pairs={{0,2},{1,3},{2,4},{3,5},{4,6},{5,7},{6,0},{7,1},{8,10},{9,11},{10,... | collective-permute-start | bytes 614408 | tf_op jit(solution)/shard_map/ppermute | solution.py:247
  5.0 4.5 %collective-permute-start.3 = (bf16[800,128]{1,0:T(8,128)(2,1)S(1)}, bf16[800,128]{1,0:T(8,128)(2,1)S(1)}, u32[]{:S(2)}, u32[]{:S(2)}) collective-permute-start(bf16[800,128]{1,0:T(8,128)(2,1)S(1)} %get-tuple-element.18.refs_3_), channel_id=1, source_target_pairs={{0,2},{1,3},{2,4},{3,5},{4,6},{5,7},{6,0},{7,1},{8,10},{9,11},{10,... | collective-permute-start | bytes 614408 | tf_op jit(solution)/shard_map/ppermute | solution.py:247
  11.1 4.5 %collective-permute-done.2.refs_6_ = bf16[800,128]{1,0:T(8,128)(2,1)S(1)} collective-permute-done((bf16[800,128]{1,0:T(8,128)(2,1)S(1)}, bf16[800,128]{1,0:T(8,128)(2,1)S(1)}, u32[]{:S(2)}, u32[]{:S(2)}) %collective-permute-start.2) | collective-permute-done | bytes 204832 | tf_op jit(solution)/shard_map/ppermute | solution.py:247
  15.6 5.4 %collective-permute-done.3.refs_7_ = bf16[800,128]{1,0:T(8,128)(2,1)S(1)} collective-permute-done((bf16[800,128]{1,0:T(8,128)(2,1)S(1)}, bf16[800,128]{1,0:T(8,128)(2,1)S(1)}, u32[]{:S(2)}, u32[]{:S(2)}) %collective-permute-start.3) | collective-permute-done | bytes 204832 | tf_op jit(solution)/shard_map/ppermute | solution.py:247
  20.9 4.5 %collective-permute-done.6.refs_10_ = bf16[800,128]{1,0:T(8,128)(2,1)S(1)} collective-permute-done((bf16[800,128]{1,0:T(8,128)(2,1)S(1)}, bf16[800,128]{1,0:T(8,128)(2,1)S(1)}, u32[]{:S(2)}, u32[]{:S(2)}) %collective-permute-start.6) | collective-permute-done | bytes 204832 | tf_op jit(solution)/shard_map/ppermute | solution.py:247
  26.4 3.4 %collective-permute-done.7.refs_11_ = bf16[800,128]{1,0:T(8,128)(2,1)S(1)} collective-permute-done((bf16[800,128]{1,0:T(8,128)(2,1)S(1)}, bf16[800,128]{1,0:T(8,128)(2,1)S(1)}, u32[]{:S(2)}, u32[]{:S(2)}) %collective-permute-start.7) | collective-permute-done | bytes 204832 | tf_op jit(solution)/shard_map/ppermute | solution.py:247
  32.7 2.6 %collective-permute-start.17 = (bf16[1600,128]{1,0:T(8,128)(2,1)S(1)}, bf16[1600,128]{1,0:T(8,128)(2,1)S(1)}, u32[]{:S(2)}, u32[]{:S(2)}) collective-permute-start(bf16[1600,128]{1,0:T(8,128)(2,1)S(1)} %slice_bitcast_fusion.refs_2_), channel_id=1, source_target_pairs={{0,6},{1,7},{2,0},{3,1},{4,2},{5,3},{6,4},{7,5},{8,14},{9,15},{10,... | collective-permute-start | bytes 1228808 | tf_op jit(solution)/shard_map/ppermute | solution.py:247
  37.0 3.9 %collective-permute-start.11 = (bf16[800,128]{1,0:T(8,128)(2,1)S(1)}, bf16[800,128]{1,0:T(8,128)(2,1)S(1)}, u32[]{:S(2)}, u32[]{:S(2)}) collective-permute-start(bf16[800,128]{1,0:T(8,128)(2,1)S(1)} %collective-permute-done.7.refs_11_), channel_id=1, source_target_pairs={{0,6},{1,7},{2,0},{3,1},{4,2},{5,3},{6,4},{7,5},{8,14},{9,15},{10,... | collective-permute-start | bytes 614408 | tf_op jit(solution)/shard_map/ppermute | solution.py:247
  42.2 18.5 %collective-permute-done.10.refs_3_ = bf16[800,128]{1,0:T(8,128)(2,1)S(1)} collective-permute-done((bf16[800,128]{1,0:T(8,128)(2,1)S(1)}, bf16[800,128]{1,0:T(8,128)(2,1)S(1)}, u32[]{:S(2)}, u32[]{:S(2)}) %collective-permute-start.10) | collective-permute-done | bytes 204832 | tf_op jit(solution)/shard_map/ppermute | solution.py:247
  69.9 2.3 %collective-permute-start.20 = (bf16[800,128]{1,0:T(8,128)(2,1)}, bf16[800,128]{1,0:T(8,128)(2,1)}, u32[]{:S(2)}, u32[]{:S(2)}) collective-permute-start(bf16[800,128]{1,0:T(8,128)(2,1)} %slice.35), channel_id=1, source_target_pairs={{0,6},{1,7},{2,0},{3,1},{4,2},{5,3},{6,4},{7,5},{8,14},{9,15},{10,... | collective-permute-start | bytes 614408 | tf_op jit(solution)/shard_map/ppermute | solution.py:247
  79.3 7.0 %shard_map.69 = (f32[400,1600]{1,0:T(8,128)S(1)}, bf16[400,1600]{1,0:T(8,128)(2,1)S(1)}) custom-call(s32[1]{0:T(128)} %shard_map.68.me, bf16[2,400,1024]{2,1,0:T(8,128)(2,1)} %bitcast.29, f32[400,1600]{1,0:T(8,128)} %bitcast.34, f32[400,1600]{1,0:T(8,128)} %bitcast.36, bf16[800,128]{1,0:T(8,128)(2,1)S(1)} %get-tuple-element.19.refs_2_, ...), custom_call_target="tpu_custom_call" | custom-call | flops 1966080000 | bytes 5120000 | tf_op jit(solution)/shard_map/pallas_call | solution.py:210
  87.0 5.2 %shard_map.70 = (bf16[5120,128]{1,0:T(8,128)(2,1)}, bf16[400,1600]{1,0:T(8,128)(2,1)}, bf16[400,1600]{1,0:T(8,128)(2,1)}) custom-call(s32[1]{0:T(128)} %bitcast.1.me, bf16[2,400,1024]{2,1,0:T(8,128)(2,1)} %bitcast.30, f32[400,1600]{1,0:T(8,128)} %bitcast.35, bf16[400,1600]{1,0:T(8,128)(2,1)S(1)} %get-tuple-element.10.refs_1_, ...), custom_call_target="tpu_custom_call" | custom-call | flops 655360000 | bytes 5120000 | tf_op jit(solution)/shard_map/pallas_call | solution.py:210
  93.5 6.9 %shard_map.71.refs_1_ = f32[400,1600]{1,0:T(8,128)} custom-call(s32[1]{0:T(128)} %bitcast.1.me, bf16[2,400,1024]{2,1,0:T(8,128)(2,1)} %bitcast.31, bf16[400,1600]{1,0:T(8,128)(2,1)S(1)} %copy-done, bf16[400,1600]{1,0:T(8,128)(2,1)} %get-tuple-element.13.refs_1_, bf16[1600,128]{1,0:T(8,128)(2,1)S(1)} %slice_bitcast_fusion.refs_2_, ...), custom_call_target="tpu_custom_call" | custom-call | flops 1966080000 | bytes 5120000 | tf_op jit(solution)/shard_map/pallas_call | solution.py:210
  100.4 4.3 %shard_map.72.moment = bf16[5120,128]{1,0:T(8,128)(2,1)} custom-call(s32[1]{0:T(128)} %bitcast.1.me, bf16[2,400,1024]{2,1,0:T(8,128)(2,1)} %bitcast.32, bf16[400,1600]{1,0:T(8,128)(2,1)S(1)} %copy-done, f32[400,1600]{1,0:T(8,128)} %shard_map.71.refs_1_, bf16[800,128]{1,0:T(8,128)(2,1)} %collective-permute-done.19.refs_2_, ...), custom_call_target="tpu_custom_call" | custom-call | flops 655360000 | bytes 5120000 | tf_op jit(solution)/shard_map/pallas_call | solution.py:210
  104.7 27.5 %all_to_all.15.got = bf16[32,160,128]{2,1,0:T(8,128)(2,1)S(1)} all-to-all(bf16[32,160,128]{2,1,0:T(8,128)(2,1)} %bitcast.33), channel_id=1, replica_groups=mesh['rep'=32,'shard'=8] {'rep'}, dimensions={0} | all-to-all | bytes 2621440 | tf_op jit(solution)/shard_map/all_to_all | solution.py:358
  132.2 4.6 %all-to-all-start.2 = ((bf16[16,320,128]{2,1,0:T(8,128)(2,1)}), bf16[16,320,128]{2,1,0:T(8,128)(2,1)S(1)}, u32[]{:S(2)}, u32[]{:S(2)}) async-start(bf16[16,320,128]{2,1,0:T(8,128)(2,1)} %bitcast.37), calls=%async_computation.2 | async-start | bytes 2621440 | tf_op jit(solution)/shard_map/all_to_all | solution.py:324
  138.1 16.8 %all-to-all-done.2.got = bf16[16,320,128]{2,1,0:T(8,128)(2,1)S(1)} async-done(((bf16[16,320,128]{2,1,0:T(8,128)(2,1)}), bf16[16,320,128]{2,1,0:T(8,128)(2,1)S(1)}, u32[]{:S(2)}, u32[]{:S(2)}) %all-to-all-start.2) | async-done | bytes 1310752 | tf_op jit(solution)/shard_map/all_to_all | solution.py:324
  154.9 5.9 %all-to-all-start.1 = ((bf16[32,160,128]{2,1,0:T(8,128)(2,1)}), bf16[32,160,128]{2,1,0:T(8,128)(2,1)S(1)}, u32[]{:S(2)}, u32[]{:S(2)}) async-start(bf16[32,160,128]{2,1,0:T(8,128)(2,1)} %shard_map.73), calls=%async_computation.1 | async-start | bytes 2621440 | tf_op jit(solution)/shard_map/all_to_all | solution.py:360
  162.5 13.9 %collective-permute-done.23.there = bf16[320,128]{1,0:T(8,128)(2,1)S(1)} collective-permute-done((bf16[320,128]{1,0:T(8,128)(2,1)S(1)}, bf16[320,128]{1,0:T(8,128)(2,1)S(1)}, u32[]{:S(2)}, u32[]{:S(2)}) %collective-permute-start.23) | collective-permute-done | bytes 81952 | tf_op jit(solution)/shard_map/ppermute | solution.py:319
  178.5 2.1 %collective-permute-start.26 = (bf16[320,128]{1,0:T(8,128)(2,1)S(1)}, bf16[320,128]{1,0:T(8,128)(2,1)S(1)}, u32[]{:S(2)}, u32[]{:S(2)}) collective-permute-start(bf16[320,128]{1,0:T(8,128)(2,1)S(1)} %shard_map.75.refs_0_), channel_id=1, source_target_pairs={{0,16},{1,129},{2,18},{3,131},{4,20},{5,133},{6,22},{7,135},{8,24}... | collective-permute-start | bytes 245768 | tf_op jit(solution)/shard_map/ppermute | solution.py:319
  182.4 2.1 %collective-permute-done.26.refs_3_ = bf16[320,128]{1,0:T(8,128)(2,1)S(1)} collective-permute-done((bf16[320,128]{1,0:T(8,128)(2,1)S(1)}, bf16[320,128]{1,0:T(8,128)(2,1)S(1)}, u32[]{:S(2)}, u32[]{:S(2)}) %collective-permute-start.26) | collective-permute-done | bytes 81952 | tf_op jit(solution)/shard_map/ppermute | solution.py:319
  190.2 2.9 %collective-permute-done.27.refs_1_ = bf16[1280,128]{1,0:T(8,128)(2,1)S(1)} collective-permute-done((bf16[1280,128]{1,0:T(8,128)(2,1)S(1)}, bf16[1280,128]{1,0:T(8,128)(2,1)S(1)}, u32[]{:S(2)}, u32[]{:S(2)}) %collective-permute-start.27) | collective-permute-done | bytes 327712 | tf_op jit(solution)/shard_map/ppermute | solution.py:319
  193.5 4.2 %collective-permute-done.29.refs_3_ = bf16[1280,128]{1,0:T(8,128)(2,1)S(1)} collective-permute-done((bf16[1280,128]{1,0:T(8,128)(2,1)S(1)}, bf16[1280,128]{1,0:T(8,128)(2,1)S(1)}, u32[]{:S(2)}, u32[]{:S(2)}) %collective-permute-start.29) | collective-permute-done | bytes 327712 | tf_op jit(solution)/shard_map/ppermute | solution.py:319
  199.7 3.7 %last.1 = (f32[400,1600]{1,0:T(8,128)}, f32[400,1600]{1,0:T(8,128)}) custom-call(f32[400,1]{1,0:T(8,128)S(1)} %copy.7.blend, bf16[5120,128]{1,0:T(8,128)(2,1)S(1)} %bitcast.28, bf16[400,1600]{1,0:T(8,128)(2,1)} %spread.1.mean_weight, bf16[5120,128]{1,0:T(8,128)(2,1)} %shard_map.72.moment), custom_call_target="tpu_custom_call" | custom-call | tf_op jit(solution)/shard_map/last/pallas_call | solution.py:371
  (106 shorter events, 42.7 us)
Async XLA Ops:
  1.7 13.9 %collective-permute-start.2 = (bf16[800,128]{1,0:T(8,128)(2,1)S(1)}, bf16[800,128]{1,0:T(8,128)(2,1)S(1)}, u32[]{:S(2)}, u32[]{:S(2)}) collective-permute-start(bf16[800,128]{1,0:T(8,128)(2,1)S(1)} %get-tuple-element.19.refs_2_), channel_id=1, source_target_pairs={{0,2},{1,3},{2,4},{3,5},{4,6},{5,7},{6,0},{7,1},{8,10},{9,11},{10,... | collective-permute-start | bytes 614408 | tf_op jit(solution)/shard_map/ppermute | solution.py:247
  5.0 15.9 %collective-permute-start.3 = (bf16[800,128]{1,0:T(8,128)(2,1)S(1)}, bf16[800,128]{1,0:T(8,128)(2,1)S(1)}, u32[]{:S(2)}, u32[]{:S(2)}) collective-permute-start(bf16[800,128]{1,0:T(8,128)(2,1)S(1)} %get-tuple-element.18.refs_3_), channel_id=1, source_target_pairs={{0,2},{1,3},{2,4},{3,5},{4,6},{5,7},{6,0},{7,1},{8,10},{9,11},{10,... | collective-permute-start | bytes 614408 | tf_op jit(solution)/shard_map/ppermute | solution.py:247
  9.5 15.9 %collective-permute-start.6 = (bf16[800,128]{1,0:T(8,128)(2,1)S(1)}, bf16[800,128]{1,0:T(8,128)(2,1)S(1)}, u32[]{:S(2)}, u32[]{:S(2)}) collective-permute-start(bf16[800,128]{1,0:T(8,128)(2,1)S(1)} %get-tuple-element.19.refs_2_), channel_id=1, source_target_pairs={{0,6},{1,7},{2,0},{3,1},{4,2},{5,3},{6,4},{7,5},{8,14},{9,15},{10,... | collective-permute-start | bytes 614408 | tf_op jit(solution)/shard_map/ppermute | solution.py:247
  9.5 20.3 %collective-permute-start.7 = (bf16[800,128]{1,0:T(8,128)(2,1)S(1)}, bf16[800,128]{1,0:T(8,128)(2,1)S(1)}, u32[]{:S(2)}, u32[]{:S(2)}) collective-permute-start(bf16[800,128]{1,0:T(8,128)(2,1)S(1)} %get-tuple-element.18.refs_3_), channel_id=1, source_target_pairs={{0,6},{1,7},{2,0},{3,1},{4,2},{5,3},{6,4},{7,5},{8,14},{9,15},{10,... | collective-permute-start | bytes 614408 | tf_op jit(solution)/shard_map/ppermute | solution.py:247
  11.1 18.8 %collective-permute-start = (bf16[800,128]{1,0:T(8,128)(2,1)S(1)}, bf16[800,128]{1,0:T(8,128)(2,1)S(1)}, u32[]{:S(2)}, u32[]{:S(2)}) collective-permute-start(bf16[800,128]{1,0:T(8,128)(2,1)S(1)} %get-tuple-element.19.refs_2_), channel_id=1, source_target_pairs={{0,1},{1,0},{2,3},{3,2},{4,5},{5,4},{6,7},{7,6},{8,9},{9,8},{10,11... | collective-permute-start | bytes 614408 | tf_op jit(solution)/shard_map/ppermute | solution.py:247
  15.6 16.5 %collective-permute-start.1 = (bf16[800,128]{1,0:T(8,128)(2,1)S(1)}, bf16[800,128]{1,0:T(8,128)(2,1)S(1)}, u32[]{:S(2)}, u32[]{:S(2)}) collective-permute-start(bf16[800,128]{1,0:T(8,128)(2,1)S(1)} %get-tuple-element.18.refs_3_), channel_id=1, source_target_pairs={{0,1},{1,0},{2,3},{3,2},{4,5},{5,4},{6,7},{7,6},{8,9},{9,8},{10,11... | collective-permute-start | bytes 614408 | tf_op jit(solution)/shard_map/ppermute | solution.py:247
  20.9 14.4 %collective-permute-start.4 = (bf16[800,128]{1,0:T(8,128)(2,1)S(1)}, bf16[800,128]{1,0:T(8,128)(2,1)S(1)}, u32[]{:S(2)}, u32[]{:S(2)}) collective-permute-start(bf16[800,128]{1,0:T(8,128)(2,1)S(1)} %collective-permute-done.2.refs_6_), channel_id=1, source_target_pairs={{0,1},{1,0},{2,3},{3,2},{4,5},{5,4},{6,7},{7,6},{8,9},{9,8},{10,11... | collective-permute-start | bytes 614408 | tf_op jit(solution)/shard_map/ppermute | solution.py:247
  25.4 10.9 %collective-permute-start.5 = (bf16[800,128]{1,0:T(8,128)(2,1)S(1)}, bf16[800,128]{1,0:T(8,128)(2,1)S(1)}, u32[]{:S(2)}, u32[]{:S(2)}) collective-permute-start(bf16[800,128]{1,0:T(8,128)(2,1)S(1)} %collective-permute-done.3.refs_7_), channel_id=1, source_target_pairs={{0,1},{1,0},{2,3},{3,2},{4,5},{5,4},{6,7},{7,6},{8,9},{9,8},{10,11... | collective-permute-start | bytes 614408 | tf_op jit(solution)/shard_map/ppermute | solution.py:247
  29.8 11.0 %collective-permute-start.8 = (bf16[800,128]{1,0:T(8,128)(2,1)S(1)}, bf16[800,128]{1,0:T(8,128)(2,1)S(1)}, u32[]{:S(2)}, u32[]{:S(2)}) collective-permute-start(bf16[800,128]{1,0:T(8,128)(2,1)S(1)} %collective-permute-done.6.refs_10_), channel_id=1, source_target_pairs={{0,1},{1,0},{2,3},{3,2},{4,5},{5,4},{6,7},{7,6},{8,9},{9,8},{10,11... | collective-permute-start | bytes 614408 | tf_op jit(solution)/shard_map/ppermute | solution.py:247
  30.5 34.3 %collective-permute-start.15 = (bf16[1600,128]{1,0:T(8,128)(2,1)S(1)}, bf16[1600,128]{1,0:T(8,128)(2,1)S(1)}, u32[]{:S(2)}, u32[]{:S(2)}) collective-permute-start(bf16[1600,128]{1,0:T(8,128)(2,1)S(1)} %slice_bitcast_fusion.refs_2_), channel_id=1, source_target_pairs={{0,2},{1,3},{2,4},{3,5},{4,6},{5,7},{6,0},{7,1},{8,10},{9,11},{10,... | collective-permute-start | bytes 1228808 | tf_op jit(solution)/shard_map/ppermute | solution.py:247
  32.7 32.1 %collective-permute-start.17 = (bf16[1600,128]{1,0:T(8,128)(2,1)S(1)}, bf16[1600,128]{1,0:T(8,128)(2,1)S(1)}, u32[]{:S(2)}, u32[]{:S(2)}) collective-permute-start(bf16[1600,128]{1,0:T(8,128)(2,1)S(1)} %slice_bitcast_fusion.refs_2_), channel_id=1, source_target_pairs={{0,6},{1,7},{2,0},{3,1},{4,2},{5,3},{6,4},{7,5},{8,14},{9,15},{10,... | collective-permute-start | bytes 1228808 | tf_op jit(solution)/shard_map/ppermute | solution.py:247
  36.0 24.7 %collective-permute-start.10 = (bf16[800,128]{1,0:T(8,128)(2,1)S(1)}, bf16[800,128]{1,0:T(8,128)(2,1)S(1)}, u32[]{:S(2)}, u32[]{:S(2)}) collective-permute-start(bf16[800,128]{1,0:T(8,128)(2,1)S(1)} %collective-permute-done.2.refs_6_), channel_id=1, source_target_pairs={{0,2},{1,3},{2,4},{3,5},{4,6},{5,7},{6,0},{7,1},{8,10},{9,11},{10,... | collective-permute-start | bytes 614408 | tf_op jit(solution)/shard_map/ppermute | solution.py:247
  37.0 25.9 %collective-permute-start.11 = (bf16[800,128]{1,0:T(8,128)(2,1)S(1)}, bf16[800,128]{1,0:T(8,128)(2,1)S(1)}, u32[]{:S(2)}, u32[]{:S(2)}) collective-permute-start(bf16[800,128]{1,0:T(8,128)(2,1)S(1)} %collective-permute-done.7.refs_11_), channel_id=1, source_target_pairs={{0,6},{1,7},{2,0},{3,1},{4,2},{5,3},{6,4},{7,5},{8,14},{9,15},{10,... | collective-permute-start | bytes 614408 | tf_op jit(solution)/shard_map/ppermute | solution.py:247
  41.6 22.0 %collective-permute-start.9 = (bf16[800,128]{1,0:T(8,128)(2,1)S(1)}, bf16[800,128]{1,0:T(8,128)(2,1)S(1)}, u32[]{:S(2)}, u32[]{:S(2)}) collective-permute-start(bf16[800,128]{1,0:T(8,128)(2,1)S(1)} %collective-permute-done.7.refs_11_), channel_id=1, source_target_pairs={{0,1},{1,0},{2,3},{3,2},{4,5},{5,4},{6,7},{7,6},{8,9},{9,8},{10,11... | collective-permute-start | bytes 614408 | tf_op jit(solution)/shard_map/ppermute | solution.py:247
  64.3 27.9 %collective-permute-start.14 = (bf16[1600,128]{1,0:T(8,128)(2,1)S(1)}, bf16[1600,128]{1,0:T(8,128)(2,1)S(1)}, u32[]{:S(2)}, u32[]{:S(2)}) collective-permute-start(bf16[1600,128]{1,0:T(8,128)(2,1)S(1)} %slice_bitcast_fusion.refs_2_), channel_id=1, source_target_pairs={{0,1},{1,0},{2,3},{3,2},{4,5},{5,4},{6,7},{7,6},{8,9},{9,8},{10,11... | collective-permute-start | bytes 1228808 | tf_op jit(solution)/shard_map/ppermute | solution.py:247
  64.8 27.4 %collective-permute-start.16 = (bf16[1600,128]{1,0:T(8,128)(2,1)S(1)}, bf16[1600,128]{1,0:T(8,128)(2,1)S(1)}, u32[]{:S(2)}, u32[]{:S(2)}) collective-permute-start(bf16[1600,128]{1,0:T(8,128)(2,1)S(1)} %collective-permute-done.15.refs_4_), channel_id=1, source_target_pairs={{0,1},{1,0},{2,3},{3,2},{4,5},{5,4},{6,7},{7,6},{8,9},{9,8},{10,11... | collective-permute-start | bytes 1228808 | tf_op jit(solution)/shard_map/ppermute | solution.py:247
  64.8 27.4 %collective-permute-start.18 = (bf16[1600,128]{1,0:T(8,128)(2,1)S(1)}, bf16[1600,128]{1,0:T(8,128)(2,1)S(1)}, u32[]{:S(2)}, u32[]{:S(2)}) collective-permute-start(bf16[1600,128]{1,0:T(8,128)(2,1)S(1)} %collective-permute-done.17.refs_6_), channel_id=1, source_target_pairs={{0,1},{1,0},{2,3},{3,2},{4,5},{5,4},{6,7},{7,6},{8,9},{9,8},{10,11... | collective-permute-start | bytes 1228808 | tf_op jit(solution)/shard_map/ppermute | solution.py:247
  67.4 18.9 %collective-permute-start.19 = (bf16[800,128]{1,0:T(8,128)(2,1)}, bf16[800,128]{1,0:T(8,128)(2,1)}, u32[]{:S(2)}, u32[]{:S(2)}) collective-permute-start(bf16[800,128]{1,0:T(8,128)(2,1)} %slice.34), channel_id=1, source_target_pairs={{0,2},{1,3},{2,4},{3,5},{4,6},{5,7},{6,0},{7,1},{8,10},{9,11},{10,... | collective-permute-start | bytes 614408 | tf_op jit(solution)/shard_map/ppermute | solution.py:247
  69.9 16.5 %collective-permute-start.20 = (bf16[800,128]{1,0:T(8,128)(2,1)}, bf16[800,128]{1,0:T(8,128)(2,1)}, u32[]{:S(2)}, u32[]{:S(2)}) collective-permute-start(bf16[800,128]{1,0:T(8,128)(2,1)} %slice.35), channel_id=1, source_target_pairs={{0,6},{1,7},{2,0},{3,1},{4,2},{5,3},{6,4},{7,5},{8,14},{9,15},{10,... | collective-permute-start | bytes 614408 | tf_op jit(solution)/shard_map/ppermute | solution.py:247
  86.3 14.1 %collective-permute-start.21 = (bf16[800,128]{1,0:T(8,128)(2,1)}, bf16[800,128]{1,0:T(8,128)(2,1)S(1)}, u32[]{:S(2)}, u32[]{:S(2)}) collective-permute-start(bf16[800,128]{1,0:T(8,128)(2,1)} %collective-permute-done.19.refs_2_), channel_id=1, source_target_pairs={{0,1},{1,0},{2,3},{3,2},{4,5},{5,4},{6,7},{7,6},{8,9},{9,8},{10,11... | collective-permute-start | bytes 614408 | tf_op jit(solution)/shard_map/ppermute | solution.py:247
  86.4 14.0 %collective-permute-start.22 = (bf16[800,128]{1,0:T(8,128)(2,1)}, bf16[800,128]{1,0:T(8,128)(2,1)S(1)}, u32[]{:S(2)}, u32[]{:S(2)}) collective-permute-start(bf16[800,128]{1,0:T(8,128)(2,1)} %collective-permute-done.20.refs_3_), channel_id=1, source_target_pairs={{0,1},{1,0},{2,3},{3,2},{4,5},{5,4},{6,7},{7,6},{8,9},{9,8},{10,11... | collective-permute-start | bytes 614408 | tf_op jit(solution)/shard_map/ppermute | solution.py:247
  132.2 22.7 %all-to-all-start.2 = ((bf16[16,320,128]{2,1,0:T(8,128)(2,1)}), bf16[16,320,128]{2,1,0:T(8,128)(2,1)S(1)}, u32[]{:S(2)}, u32[]{:S(2)}) async-start(bf16[16,320,128]{2,1,0:T(8,128)(2,1)} %bitcast.37), calls=%async_computation.2 | async-start | bytes 2621440 | tf_op jit(solution)/shard_map/all_to_all | solution.py:324
  154.9 44.8 %all-to-all-start.1 = ((bf16[32,160,128]{2,1,0:T(8,128)(2,1)}), bf16[32,160,128]{2,1,0:T(8,128)(2,1)S(1)}, u32[]{:S(2)}, u32[]{:S(2)}) async-start(bf16[32,160,128]{2,1,0:T(8,128)(2,1)} %shard_map.73), calls=%async_computation.1 | async-start | bytes 2621440 | tf_op jit(solution)/shard_map/all_to_all | solution.py:360
  161.0 15.4 %collective-permute-start.23 = (bf16[320,128]{1,0:T(8,128)(2,1)S(1)}, bf16[320,128]{1,0:T(8,128)(2,1)S(1)}, u32[]{:S(2)}, u32[]{:S(2)}) collective-permute-start(bf16[320,128]{1,0:T(8,128)(2,1)S(1)} %shard_map.74.here), channel_id=1, source_target_pairs={{0,32},{1,33},{2,34},{3,35},{4,36},{5,37},{6,38},{7,39},{8,40},{9,... | collective-permute-start | bytes 245768 | tf_op jit(solution)/shard_map/ppermute | solution.py:319
  (32 other events, 127.8 us)

commit v2 on v1

--- a/solution.py
+++ b/solution.py
@@ -29,9 +29,9 @@
     return (pre * half - wanted) * deriv * SCALE
 
 
-def places(me, ups):
+def places(me, ups, apart):
     z, c = me // 2, me % 2
-    return [2 * ((z + up) % 4) + (c + k) % 2 for up in ups for k in range(2)]
+    return [2 * ((z + (up * (2 * q - 1) if apart else up) + 8) % 4) + q for up in ups for q in (c, 1 - c)]
 
 
 UNITS = 80
@@ -64,68 +64,66 @@
     def kernel(me, wanted, *refs):
         extra = 4 if first and late else 1
         refs, (x, g, m_buf, want, fetched, loaded, stored, *bufs) = refs[: -7 - extra], refs[-7 - extra :]
-        if first and late:
-            full, half, moment, *refs = refs
-        elif first:
-            full, moment, *refs = refs
-        else:
-            half, moment, *refs = refs
-        count = 2 * len(ups) * (1 if step and not late else 2)
+        full = half = None
+        if first:
+            full, *refs = refs
+        if late or not first:
+            half, *refs = refs
+        moment, *refs = refs
+        count = 2 * len(ups) * (2 - step)
         blocks, outs = refs[:count], refs[count:]
         units = wanted.shape[1]
-        lines, w_buf, w_half, m_half = bufs if len(bufs) == 4 else (bufs[0], bufs[0], None, None)
-        loads = []
-        if first:
-            loads.append(pltpu.make_async_copy(full, w_buf, loaded.at[0]))
-        if not (first and late):
-            loads.append(pltpu.make_async_copy(moment, m_buf, loaded.at[1]))
         fetches = []
-        for i, a in enumerate(places(me[0], ups)):
+        for i, a in enumerate(places(me[0], ups, step == 1)):
             lanes = slice(i * LANES, (i + 1) * LANES)
-            theirs = wanted.at[step, :, pl.ds(pl.multiple_of(a * LANES, LANES), LANES)]
-            moves = [(theirs, want.at[:, lanes])]
+            moves = [(wanted.at[step, :, pl.ds(pl.multiple_of(a * LANES, LANES), LANES)], want.at[:, lanes])]
             if count == 2 * len(ups):
                 moves.append((blocks[i], x.at[:, lanes]))
             else:
                 moves += [(blocks[2 * i], x.at[:TOP, lanes]), (blocks[2 * i + 1], x.at[TOP:, lanes])]
-            for k, (part, whole) in enumerate(moves):
-                fetches.append(pltpu.make_async_copy(part, whole, fetched.at[i, k]))
+            fetches.append([pltpu.make_async_copy(*m, fetched.at[i, k]) for k, m in enumerate(moves)])
+        loads = []
+        if first:
+            w_buf = bufs[1 if late else 0]
+            loads.append(pltpu.make_async_copy(full, w_buf, loaded.at[0]))
+        if not late:
+            loads.append(pltpu.make_async_copy(moment, m_buf, loaded.at[1]))
         if first and not late:
             loads[0].start()
         for fetch in fetches:
-            fetch.start()
+            for copy in fetch:
+                copy.start()
         for load in loads[first and not late :]:
             load.start()
-        for fetch in fetches:
-            fetch.wait()
         if first and not late:
-            loads[0].wait()
+            loads.pop(0).wait()
             half = outs[1]
             half[...] = w_buf[...].astype(jnp.bfloat16)
+        for fetch in fetches:
+            for copy in fetch:
+                copy.wait()
         pre = jnp.dot(half[...], x[...], preferred_element_type=jnp.float32) * SCALE
         hidden = slope(pre, want[...].astype(jnp.float32)).astype(jnp.bfloat16)
-        g[...] = lax.dot_general(hidden, x[...], (((1,), (1,)), ((), ())), preferred_element_type=jnp.float32)
-        for load in loads[first and not late :]:
+        for load in loads:
             load.wait()
+        grad = lax.dot_general(hidden, x[...], (((1,), (1,)), ((), ())), preferred_element_type=jnp.float32)
+        if not late:
+            outs[0][...] = DECAY * m_buf[...].astype(jnp.float32) + grad
+            return
+        g[...] = grad
+        lines = bufs[0]
         copies = []
         for i in range(units // UNITS):
             rows, span = slice(i * UNITS, (i + 1) * UNITS), slice(i * LINES, (i + 1) * LINES)
-            if first and late:
-                m = moment[rows, :] + g[rows, :]
-                w = w_buf[rows, :] - LEARN * m
-                w_half[rows, :] = w.astype(jnp.bfloat16)
+            m = moment[rows, :] + g[rows, :]
+            moves = [(lines, span)]
+            if first:
+                _, w_buf, w_half, m_half = bufs
+                w_half[rows, :] = (w_buf[rows, :] - LEARN * m).astype(jnp.bfloat16)
                 m_half[rows, :] = m.astype(jnp.bfloat16)
-                pack(lines.at[span, :], w)
-                moves = [(lines, span), (w_half, rows), (m_half, rows)]
-            elif first:
-                outs[0][rows, :] = DECAY * m_buf[rows, :] + g[rows, :]
-                moves = []
-            elif late:
-                pack(lines.at[span, :], m_buf[rows, :] + g[rows, :])
-                moves = [(lines, span)]
-            else:
-                g[rows, :] = DECAY * m_buf[rows, :].astype(jnp.float32) + g[rows, :]
-                moves = [(g, rows)]
+                moves += [(w_half, rows), (m_half, rows)]
+                m = w_half[rows, :]
+            pack(lines.at[span, :], m)
             for o, (buf, part) in enumerate(moves):
                 copy = pltpu.make_async_copy(buf.at[part, :], outs[o].at[part, :], stored.at[o, i])
                 copy.start()
@@ -136,30 +134,26 @@
     return kernel
 
 
-def last_kernel(blend, lines, mean_weight, moment, averaged, blended, m_buf, w_buf, a_buf, b_buf, loaded, stored):
-    loads, copies = [], []
-    count = averaged.shape[0] // UNITS
-    parts = [(slice(i * UNITS, (i + 1) * UNITS), slice(i * LINES, (i + 1) * LINES)) for i in range(count)]
-    for i, (rows, span) in enumerate(parts):
-        loads.append(
-            [
-                pltpu.make_async_copy(mean_weight.at[rows, :], w_buf.at[rows, :], loaded.at[0, i]),
-                pltpu.make_async_copy(moment.at[span, :], m_buf.at[span, :], loaded.at[1, i]),
-            ]
-        )
-        for load in loads[-1]:
-            load.start()
-    for i, (rows, span) in enumerate(parts):
-        for load in loads[i]:
-            load.wait()
+def put_out(buf, out, rows, sem):
+    copy = pltpu.make_async_copy(buf.at[rows, :], out.at[rows, :], sem)
+    copy.start()
+    return copy
+
+
+def blend_kernel(blend, lines, moment, blended, m_buf, b_buf, loaded, stored):
+    count = blended.shape[0] // UNITS
+    spans = [slice(i * LINES, (i + 1) * LINES) for i in range(count)]
+    loads = [pltpu.make_async_copy(moment.at[p, :], m_buf.at[p, :], loaded.at[i]) for i, p in enumerate(spans)]
+    for load in loads:
+        load.start()
+    copies = []
+    for i in range(count):
+        loads[i].wait()
+        rows = slice(i * UNITS, (i + 1) * UNITS)
         b = blend[rows, :]
         for (lanes, m), (_, own) in zip(unpacked(lines, i * LINES), unpacked(m_buf, i * LINES)):
-            a_buf[rows, lanes] = w_buf[rows, lanes].astype(jnp.float32) - LEARN * m
             b_buf[rows, lanes] = b * m + (1.0 - b) * own
-        for k, (buf, out) in enumerate([(a_buf, averaged), (b_buf, blended)]):
-            copy = pltpu.make_async_copy(buf.at[rows, :], out.at[rows, :], stored.at[k, i])
-            copy.start()
-            copies.append(copy)
+        copies.append(put_out(b_buf, blended, rows, stored.at[i]))
     for copy in copies:
         copy.wait()
 
@@ -167,18 +161,23 @@
 ROUND = (0, 3, 1, 2)
 
 
-def spread_kernel(me, *refs):
-    *parts, out, lines = refs
-    x, y, core = me[0] // 8, me[0] % 4, me[1] % 2
-    rows = lines.shape[0] // 16
+def average_kernel(rep, me, lines, *refs):
+    *parts, averaged, w_lines, a_buf, stored = refs
+    x, y, core = rep[0] // 8, rep[0] % 4, me[0] % 2
+    chunk = lines.shape[0] // 16
     for part, far in zip(parts, ROUND):
         for i, near in enumerate(ROUND):
             dx, dy = near + core * (far - near), far + core * (near - far)
             owner = (x + dy) % 4 * 4 + (y + dx) % 4
-            lines[pl.ds(pl.multiple_of(owner * rows, rows), rows), :] = part[i * rows : (i + 1) * rows, :]
-    for u in range(out.shape[0] // UNITS):
-        for lanes, v in unpacked(lines, u * LINES):
-            out[u * UNITS : (u + 1) * UNITS, lanes] = v.astype(jnp.bfloat16)
+            w_lines[pl.ds(pl.multiple_of(owner * chunk, chunk), chunk), :] = part[i * chunk : (i + 1) * chunk, :]
+    copies = []
+    for i in range(averaged.shape[0] // UNITS):
+        rows = slice(i * UNITS, (i + 1) * UNITS)
+        for (lanes, w), (_, m) in zip(unpacked(w_lines, i * LINES), unpacked(lines, i * LINES)):
+            a_buf[rows, lanes] = w - LEARN * m
+        copies.append(put_out(a_buf, averaged, rows, stored.at[i]))
+    for copy in copies:
+        copy.wait()
 
 
 SMEM = pl.BlockSpec(memory_space=pltpu.SMEM)
@@ -199,23 +198,23 @@
     whole, half = ((units, D), jnp.float32), ((units, D), jnp.bfloat16)
     lines = (units // UNITS * LINES, LANES), jnp.bfloat16
     outs = [[[whole], [lines]], [[whole, half], [lines, half, half]]][first][late]
-    bufs = [lines if late else whole if first else ((8, LANES), jnp.bfloat16)]
+    small = (8, LANES), jnp.float32
+    bufs = [lines if late else whole if first else small]
     if first and late:
         bufs = [lines, whole, half, half]
-    here = first and not late
     args = [kept(w) if w.dtype == jnp.float32 else w for w in weights]
     specs = [FAR if w.dtype == jnp.float32 else VMEM for w in weights]
-    args.append(moment if first and late else kept(moment))
-    specs.append(VMEM if first and late else FAR)
+    args.append(moment if late else kept(moment))
+    specs.append(VMEM if late else FAR)
     return pl.pallas_call(
         step_kernel(step, ups, late),
-        out_shape=tuple(jax.ShapeDtypeStruct(*o) if here else pltpu.HBM(*o) for o in outs),
+        out_shape=tuple((pltpu.HBM if late else jax.ShapeDtypeStruct)(*o) for o in outs),
         in_specs=[SMEM, FAR, *specs] + [pl.BlockSpec(memory_space=pl.ANY)] * len(blocks),
-        out_specs=(VMEM if here else FAR,) * len(outs),
+        out_specs=(FAR if late else VMEM,) * len(outs),
         scratch_shapes=[
             pltpu.VMEM((D, tokens), jnp.bfloat16),
-            pltpu.VMEM(*whole),
-            pltpu.VMEM(moment.shape, moment.dtype),
+            pltpu.VMEM(*(whole if late else small)),
+            pltpu.VMEM(*(small if late else (moment.shape, moment.dtype))),
             pltpu.VMEM((units, tokens), jnp.bfloat16),
             pltpu.SemaphoreType.DMA((2 * len(ups), 3)),
             pltpu.SemaphoreType.DMA((2,)),
@@ -258,12 +257,17 @@
 
 
 def gather_whole(piece):
-    low, high = shard_permute(piece, 1, 0), shard_permute(piece, -1, 0)
-    far = [shard_permute(low[:TOP], 1, 0), shard_permute(high[TOP:], -1, 0)]
+    def passed(v, up):
+        pairs = [(2 * z + c, 2 * ((z + up * (1 - 2 * c)) % 4) + c) for z in range(4) for c in range(2)]
+        return lax.ppermute(v, "shard", pairs)
+
+    one = passed(piece, 1)
+    back = passed(piece, -1)
+    two = passed(one, 1)
     near = []
-    for v in (piece, low, high):
+    for v in (piece, one, back):
         near += [v, shard_permute(v, 0, 1)]
-    return near, both_cores(far)
+    return near, [two, shard_permute(two, 0, 1)]
 
 
 def both_cores(values):
@@ -342,10 +346,10 @@
     rows = units // UNITS * LINES
 
     whole = jax.ShapeDtypeStruct((units, D), jnp.float32)
-    half = jax.ShapeDtypeStruct((units, D), jnp.bfloat16)
 
     near, far, sent = gather(pieces[0])
-    second, _ = lax.optimization_barrier((pieces[1], sent))
+    second = pieces[1]
+    second, _ = lax.optimization_barrier((second, sent))
     near2, far2 = gather_whole(second)
 
     ready = gate(me)
@@ -353,37 +357,39 @@
     weight_lines, weight, moment = local_step(me, wanted, [weight, old], moment, far, 0, (2,))
     parts = weight_mean(weight_lines)
 
-    (moment,) = local_step(me, wanted, [weight], moment, near2, 1, (0, 3, 1))
+    (moment,) = local_step(me, wanted, [weight], moment, near2, 1, (0, 1, -1))
     (moment_lines,) = local_step(me, wanted, [weight], moment, far2, 1, (2,))
     got = lax.all_to_all(moment_lines.reshape(replicas, -1, LANES), "rep", 0, 0)
     means = small(mean_kernel, [got], got.shape)
     mean_moment = lax.all_to_all(means, "rep", 0, 0).reshape(-1, LANES)
 
-    mean_weight = pl.pallas_call(
-        spread_kernel,
-        out_shape=pltpu.HBM(half.shape, half.dtype),
-        in_specs=[SMEM] + [VMEM] * 4,
-        out_specs=VMEM,
-        scratch_shapes=[pltpu.VMEM((rows, LANES), jnp.bfloat16)],
-        compiler_params=pltpu.CompilerParams(vmem_limit_bytes=12 * MIB),
-        name="spread",
-    )(jnp.stack([lax.axis_index("rep"), lax.axis_index("shard")]), *parts)
-    averaged, blended = pl.pallas_call(
-        last_kernel,
-        out_shape=(whole, whole),
-        in_specs=[VMEM, VMEM, FAR, FAR],
-        out_specs=(FAR, FAR),
+    blended = pl.pallas_call(
+        blend_kernel,
+        out_shape=whole,
+        in_specs=[VMEM, VMEM, FAR],
+        out_specs=FAR,
         scratch_shapes=[
             pltpu.VMEM((rows, LANES), jnp.bfloat16),
-            pltpu.VMEM((units, D), jnp.bfloat16),
             pltpu.VMEM((units, D), jnp.float32),
+            pltpu.SemaphoreType.DMA((units // UNITS,)),
+            pltpu.SemaphoreType.DMA((units // UNITS,)),
+        ],
+        compiler_params=pltpu.CompilerParams(vmem_limit_bytes=12 * MIB),
+        name="blended",
+    )(blend_weight[:, None], mean_moment, kept(moment_lines))
+    averaged = pl.pallas_call(
+        average_kernel,
+        out_shape=whole,
+        in_specs=[SMEM, SMEM] + [VMEM] * 5,
+        out_specs=FAR,
+        scratch_shapes=[
+            pltpu.VMEM((rows, LANES), jnp.bfloat16),
             pltpu.VMEM((units, D), jnp.float32),
-            pltpu.SemaphoreType.DMA((2, units // UNITS)),
-            pltpu.SemaphoreType.DMA((2, units // UNITS)),
+            pltpu.SemaphoreType.DMA((units // UNITS,)),
         ],
-        compiler_params=pltpu.CompilerParams(vmem_limit_bytes=16 * MIB),
-        name="last",
-    )(blend_weight[:, None], mean_moment, kept(mean_weight), kept(moment_lines))
+        compiler_params=pltpu.CompilerParams(vmem_limit_bytes=12 * MIB),
+        name="averaged",
+    )(gate(lax.axis_index("rep")[None]), me, mean_moment, *parts)
     return averaged.T, blended.T[None]
 
 

time: 206 us -> 213 us (1.034)
  starting transfers between devices: 45.1 us -> 64.9 us
  waiting for transfers between devices: 79.8 us -> 67.3 us
    ppermute x0 -> x3, starting transfers between devices: none -> 25.4 us  [passed(): return lax.ppermute(v, 'shard', pairs)]
    ppermute x23 -> x18, waiting for transfers between devices: 37.7 us -> 27.9 us  [shard_permute(): return lax.ppermute(v, 'shard', rotated(up, cores))]
    ppermute x23 -> x18, starting transfers between devices: 23.4 us -> 17.5 us  [shard_permute(): return lax.ppermute(v, 'shard', rotated(up, cores))]
    ppermute x7, waiting for transfers between devices: 25.3 us -> 22.3 us  [replica_permute(): return lax.ppermute(v, ('rep', 'shard'), pairs)]
    pallas_call x6, Pallas kernels: 29.1 us -> 26.8 us  [the longest x4 21.7 us: local_step(): pl.pallas_call(step_kernel(step, ups, late), out_shape=tuple(((pltpu.HBM...]
  transfers between devices with their start and end apart: 32 -> 30, of which waited for: 14 -> 11; matrix products, arithmetic and copies ran while one was open for 1% -> 1% of each run, Pallas kernels for 11% -> 11%
where the time goes in v2:
time: 213 us; the launch traced here: 210 us
  waiting for transfers between devices  67.3 us (32%)
  starting transfers between devices  64.9 us (30%)
  Pallas kernels  29.3 us (14%)
  blocking collectives  27.7 us (13%)
  local copies, waits for them, and re-layouts  19.4 us (9%)
    ppermute x18, waiting for transfers between devices, shard_permute(): return lax.ppermute(v, 'shard', rotated(up, cores))  27.9 us
    all_to_all x1, blocking collectives, body(): got = lax.all_to_all(moment_lines.reshape(replicas, -1, LANES), 'rep', 0, 0)  27.7 us
    ppermute x3, starting transfers between devices, passed(): return lax.ppermute(v, 'shard', pairs)  25.4 us
    ppermute x7, waiting for transfers between devices, replica_permute(): return lax.ppermute(v, ('rep', 'shard'), pairs)  22.3 us
    pallas_call x4, Pallas kernels, local_step(): pl.pallas_call(step_kernel(step, ups, late), out_shape=tuple(((pltpu.HBM...  21.7 us
    ppermute x18, starting transfers between devices, shard_permute(): return lax.ppermute(v, 'shard', rotated(up, cores))  17.5 us
    unnamed x48, local copies, waits for them, and re-layouts  17.2 us
    all_to_all x1, waiting for transfers between devices, weight_mean(): lax.all_to_all(lines.reshape(16, -1, LANES), 'rep', 0, 0, axis_index_grou...  17.1 us
  transfers between devices with their start and end apart: 30, of which 11 were waited for; matrix products, arithmetic and copies ran while one was open for 1% of the time, Pallas kernels for 11%

profile of v2, /device:TPU:8, one launch (start us, length us, event | category | flops | bytes accessed | tf_op | source)
XLA Modules:
  0.0 209.7 jit_solution(14650895108139634614)
XLA Ops:
  1.7 3.3 %collective-permute-start.2 = (bf16[800,128]{1,0:T(8,128)(2,1)S(1)}, bf16[800,128]{1,0:T(8,128)(2,1)S(1)}, u32[]{:S(2)}, u32[]{:S(2)}) collective-permute-start(bf16[800,128]{1,0:T(8,128)(2,1)S(1)} %get-tuple-element.15.refs_2_), channel_id=1, source_target_pairs={{0,2},{1,3},{2,4},{3,5},{4,6},{5,7},{6,0},{7,1},{8,10},{9,11},{10,... | collective-permute-start | bytes 614408 | tf_op jit(solution)/shard_map/ppermute | solution.py:246
  5.0 3.1 %collective-permute-start.6 = (bf16[800,128]{1,0:T(8,128)(2,1)S(1)}, bf16[800,128]{1,0:T(8,128)(2,1)S(1)}, u32[]{:S(2)}, u32[]{:S(2)}) collective-permute-start(bf16[800,128]{1,0:T(8,128)(2,1)S(1)} %get-tuple-element.15.refs_2_), channel_id=1, source_target_pairs={{0,6},{1,7},{2,0},{3,1},{4,2},{5,3},{6,4},{7,5},{8,14},{9,15},{10,... | collective-permute-start | bytes 614408 | tf_op jit(solution)/shard_map/ppermute | solution.py:246
  10.6 10.4 %collective-permute-done.3.refs_7_ = bf16[800,128]{1,0:T(8,128)(2,1)S(1)} collective-permute-done((bf16[800,128]{1,0:T(8,128)(2,1)S(1)}, bf16[800,128]{1,0:T(8,128)(2,1)S(1)}, u32[]{:S(2)}, u32[]{:S(2)}) %collective-permute-start.3) | collective-permute-done | bytes 204832 | tf_op jit(solution)/shard_map/ppermute | solution.py:246
  20.9 6.0 %collective-permute-start.15 = (bf16[1600,128]{1,0:T(8,128)(2,1)S(1)}, bf16[1600,128]{1,0:T(8,128)(2,1)S(1)}, u32[]{:S(2)}, u32[]{:S(2)}) collective-permute-start(bf16[1600,128]{1,0:T(8,128)(2,1)S(1)} %slice_bitcast_fusion.refs_2_), channel_id=1, source_target_pairs={{0,2},{1,7},{2,4},{3,1},{4,6},{5,3},{6,0},{7,5},{8,10},{9,15},{10,... | collective-permute-start | bytes 1228808 | tf_op jit(solution)/shard_map/ppermute | solution.py:262
  26.9 2.1 collective-permute-start.7
  31.0 12.1 %collective-permute-done.7.refs_11_ = bf16[800,128]{1,0:T(8,128)(2,1)S(1)} collective-permute-done((bf16[800,128]{1,0:T(8,128)(2,1)S(1)}, bf16[800,128]{1,0:T(8,128)(2,1)S(1)}, u32[]{:S(2)}, u32[]{:S(2)}) %collective-permute-start.7) | collective-permute-done | bytes 204832 | tf_op jit(solution)/shard_map/ppermute | solution.py:246
  47.5 16.3 %collective-permute-start.17 = (bf16[1600,128]{1,0:T(8,128)(2,1)S(1)}, bf16[1600,128]{1,0:T(8,128)(2,1)S(1)}, u32[]{:S(2)}, u32[]{:S(2)}) collective-permute-start(bf16[1600,128]{1,0:T(8,128)(2,1)S(1)} %slice_bitcast_fusion.refs_2_), channel_id=1, source_target_pairs={{0,6},{1,3},{2,0},{3,5},{4,2},{5,7},{6,4},{7,1},{8,14},{9,11},{10,... | collective-permute-start | bytes 1228808 | tf_op jit(solution)/shard_map/ppermute | solution.py:262
  64.5 3.1 %collective-permute-start.19 = (bf16[1600,128]{1,0:T(8,128)(2,1)S(1)}, bf16[1600,128]{1,0:T(8,128)(2,1)S(1)}, u32[]{:S(2)}, u32[]{:S(2)}) collective-permute-start(bf16[1600,128]{1,0:T(8,128)(2,1)S(1)} %collective-permute-done.15.refs_4_), channel_id=1, source_target_pairs={{0,2},{1,7},{2,4},{3,1},{4,6},{5,3},{6,0},{7,5},{8,10},{9,15},{10,... | collective-permute-start | bytes 1228808 | tf_op jit(solution)/shard_map/ppermute | solution.py:262
  70.7 3.2 %collective-permute-done.10.refs_3_ = bf16[800,128]{1,0:T(8,128)(2,1)S(1)} collective-permute-done((bf16[800,128]{1,0:T(8,128)(2,1)S(1)}, bf16[800,128]{1,0:T(8,128)(2,1)S(1)}, u32[]{:S(2)}, u32[]{:S(2)}) %collective-permute-start.10) | collective-permute-done | bytes 204832 | tf_op jit(solution)/shard_map/ppermute | solution.py:246
  75.8 2.2 %collective-permute-done.11.refs_4_ = bf16[800,128]{1,0:T(8,128)(2,1)} collective-permute-done((bf16[800,128]{1,0:T(8,128)(2,1)S(1)}, bf16[800,128]{1,0:T(8,128)(2,1)}, u32[]{:S(2)}, u32[]{:S(2)}) %collective-permute-start.11) | collective-permute-done | bytes 204832 | tf_op jit(solution)/shard_map/ppermute | solution.py:246
  89.9 6.8 %shard_map.70 = (f32[400,1600]{1,0:T(8,128)S(1)}, bf16[400,1600]{1,0:T(8,128)(2,1)S(1)}) custom-call(s32[1]{0:T(128)} %shard_map.69.me, bf16[2,400,1024]{2,1,0:T(8,128)(2,1)} %bitcast.30, f32[400,1600]{1,0:T(8,128)} %bitcast.35, f32[400,1600]{1,0:T(8,128)} %bitcast.37, bf16[800,128]{1,0:T(8,128)(2,1)S(1)} %get-tuple-element.15.refs_2_, ...), custom_call_target="tpu_custom_call" | custom-call | flops 1966080000 | bytes 5120000 | tf_op jit(solution)/shard_map/pallas_call | solution.py:209
  96.7 5.3 %shard_map.71 = (bf16[5120,128]{1,0:T(8,128)(2,1)}, bf16[400,1600]{1,0:T(8,128)(2,1)}, bf16[400,1600]{1,0:T(8,128)(2,1)}) custom-call(s32[1]{0:T(128)} %bitcast.1.me, bf16[2,400,1024]{2,1,0:T(8,128)(2,1)} %bitcast.31, f32[400,1600]{1,0:T(8,128)} %bitcast.36, bf16[400,1600]{1,0:T(8,128)(2,1)S(1)} %get-tuple-element.8.refs_1_, ...), custom_call_target="tpu_custom_call" | custom-call | flops 655360000 | bytes 5120000 | tf_op jit(solution)/shard_map/pallas_call | solution.py:209
  103.5 5.5 %shard_map.72.refs_1_ = f32[400,1600]{1,0:T(8,128)S(1)} custom-call(s32[1]{0:T(128)} %bitcast.1.me, bf16[2,400,1024]{2,1,0:T(8,128)(2,1)} %bitcast.32, bf16[400,1600]{1,0:T(8,128)(2,1)S(1)} %copy-done, bf16[400,1600]{1,0:T(8,128)(2,1)} %get-tuple-element.11.refs_1_, bf16[1600,128]{1,0:T(8,128)(2,1)S(1)} %slice_bitcast_fusion.refs_2_, ...), custom_call_target="tpu_custom_call" | custom-call | flops 1966080000 | bytes 5120000 | tf_op jit(solution)/shard_map/pallas_call | solution.py:209
  109.0 4.1 %shard_map.73.moment = bf16[5120,128]{1,0:T(8,128)(2,1)} custom-call(s32[1]{0:T(128)} %bitcast.1.me, bf16[2,400,1024]{2,1,0:T(8,128)(2,1)} %bitcast.33, bf16[400,1600]{1,0:T(8,128)(2,1)S(1)} %copy-done, f32[400,1600]{1,0:T(8,128)S(1)} %shard_map.72.refs_1_, bf16[1600,128]{1,0:T(8,128)(2,1)S(1)} %collective-permute-done.19.refs_2_, ...), custom_call_target="tpu_custom_call" | custom-call | flops 655360000 | bytes 5120000 | tf_op jit(solution)/shard_map/pallas_call | solution.py:209
  113.0 27.7 %all_to_all.15.got = bf16[32,160,128]{2,1,0:T(8,128)(2,1)S(1)} all-to-all(bf16[32,160,128]{2,1,0:T(8,128)(2,1)} %bitcast.34), channel_id=1, replica_groups=mesh['rep'=32,'shard'=8] {'rep'}, dimensions={0} | all-to-all | bytes 2621440 | tf_op jit(solution)/shard_map/all_to_all | solution.py:362
  140.8 4.6 %all-to-all-start.2 = ((bf16[16,320,128]{2,1,0:T(8,128)(2,1)}), bf16[16,320,128]{2,1,0:T(8,128)(2,1)S(1)}, u32[]{:S(2)}, u32[]{:S(2)}) async-start(bf16[16,320,128]{2,1,0:T(8,128)(2,1)} %bitcast.40), calls=%async_computation.2 | async-start | bytes 2621440 | tf_op jit(solution)/shard_map/all_to_all | solution.py:328
  146.6 17.1 %all-to-all-done.2.got = bf16[16,320,128]{2,1,0:T(8,128)(2,1)S(1)} async-done(((bf16[16,320,128]{2,1,0:T(8,128)(2,1)}), bf16[16,320,128]{2,1,0:T(8,128)(2,1)S(1)}, u32[]{:S(2)}, u32[]{:S(2)}) %all-to-all-start.2) | async-done | bytes 1310752 | tf_op jit(solution)/shard_map/all_to_all | solution.py:328
  163.7 6.4 %all-to-all-start.1 = ((bf16[32,160,128]{2,1,0:T(8,128)(2,1)}), bf16[32,160,128]{2,1,0:T(8,128)(2,1)S(1)}, u32[]{:S(2)}, u32[]{:S(2)}) async-start(bf16[32,160,128]{2,1,0:T(8,128)(2,1)} %shard_map.74), calls=%async_computation.1 | async-start | bytes 2621440 | tf_op jit(solution)/shard_map/all_to_all | solution.py:364
  171.9 14.1 %collective-permute-done.21.there = bf16[320,128]{1,0:T(8,128)(2,1)S(1)} collective-permute-done((bf16[320,128]{1,0:T(8,128)(2,1)S(1)}, bf16[320,128]{1,0:T(8,128)(2,1)S(1)}, u32[]{:S(2)}, u32[]{:S(2)}) %collective-permute-start.21) | collective-permute-done | bytes 81952 | tf_op jit(solution)/shard_map/ppermute | solution.py:323
  188.2 2.1 collective-permute-start.24
  192.1 2.1 collective-permute-done.24.refs_3_
  200.1 2.7 %blended.1 = f32[400,1600]{1,0:T(8,128)} custom-call(f32[400,1]{1,0:T(8,128)S(1)} %copy.7.blend, bf16[5120,128]{1,0:T(8,128)(2,1)S(1)} %bitcast.28, bf16[5120,128]{1,0:T(8,128)(2,1)} %shard_map.73.moment), custom_call_target="tpu_custom_call" | custom-call | tf_op jit(solution)/shard_map/blended/pallas_call | solution.py:366
  202.9 4.2 %collective-permute-done.27.refs_3_ = bf16[1280,128]{1,0:T(8,128)(2,1)S(1)} collective-permute-done((bf16[1280,128]{1,0:T(8,128)(2,1)S(1)}, bf16[1280,128]{1,0:T(8,128)(2,1)S(1)}, u32[]{:S(2)}, u32[]{:S(2)}) %collective-permute-start.27) | collective-permute-done | bytes 327712 | tf_op jit(solution)/shard_map/ppermute | solution.py:323
  207.1 2.4 %averaged.1 = f32[400,1600]{1,0:T(8,128)} custom-call(s32[1]{0:T(128)} %shard_map.68.rep, s32[1]{0:T(128)} %bitcast.1.me, bf16[5120,128]{1,0:T(8,128)(2,1)S(1)} %bitcast.29, bf16[1280,128]{1,0:T(8,128)(2,1)S(1)} %shard_map.77.refs_0_, bf16[1280,128]{1,0:T(8,128)(2,1)S(1)} %collective-permute-done.25.refs_1_, ...), custom_call_target="tpu_custom_call" | custom-call | tf_op jit(solution)/shard_map/averaged/pallas_call | solution.py:380
  (100 shorter events, 41.8 us)
Async XLA Ops:
  1.7 28.8 %collective-permute-start.2 = (bf16[800,128]{1,0:T(8,128)(2,1)S(1)}, bf16[800,128]{1,0:T(8,128)(2,1)S(1)}, u32[]{:S(2)}, u32[]{:S(2)}) collective-permute-start(bf16[800,128]{1,0:T(8,128)(2,1)S(1)} %get-tuple-element.15.refs_2_), channel_id=1, source_target_pairs={{0,2},{1,3},{2,4},{3,5},{4,6},{5,7},{6,0},{7,1},{8,10},{9,11},{10,... | collective-permute-start | bytes 614408 | tf_op jit(solution)/shard_map/ppermute | solution.py:246
  5.0 15.9 %collective-permute-start.6 = (bf16[800,128]{1,0:T(8,128)(2,1)S(1)}, bf16[800,128]{1,0:T(8,128)(2,1)S(1)}, u32[]{:S(2)}, u32[]{:S(2)}) collective-permute-start(bf16[800,128]{1,0:T(8,128)(2,1)S(1)} %get-tuple-element.15.refs_2_), channel_id=1, source_target_pairs={{0,6},{1,7},{2,0},{3,1},{4,2},{5,3},{6,4},{7,5},{8,14},{9,15},{10,... | collective-permute-start | bytes 614408 | tf_op jit(solution)/shard_map/ppermute | solution.py:246
  8.2 12.8 %collective-permute-start.3 = (bf16[800,128]{1,0:T(8,128)(2,1)S(1)}, bf16[800,128]{1,0:T(8,128)(2,1)S(1)}, u32[]{:S(2)}, u32[]{:S(2)}) collective-permute-start(bf16[800,128]{1,0:T(8,128)(2,1)S(1)} %get-tuple-element.14.refs_3_), channel_id=1, source_target_pairs={{0,2},{1,3},{2,4},{3,5},{4,6},{5,7},{6,0},{7,1},{8,10},{9,11},{10,... | collective-permute-start | bytes 614408 | tf_op jit(solution)/shard_map/ppermute | solution.py:246
  20.9 43.5 %collective-permute-start.15 = (bf16[1600,128]{1,0:T(8,128)(2,1)S(1)}, bf16[1600,128]{1,0:T(8,128)(2,1)S(1)}, u32[]{:S(2)}, u32[]{:S(2)}) collective-permute-start(bf16[1600,128]{1,0:T(8,128)(2,1)S(1)} %slice_bitcast_fusion.refs_2_), channel_id=1, source_target_pairs={{0,2},{1,7},{2,4},{3,1},{4,6},{5,3},{6,0},{7,5},{8,10},{9,15},{10,... | collective-permute-start | bytes 1228808 | tf_op jit(solution)/shard_map/ppermute | solution.py:262
  26.9 16.2 %collective-permute-start.7 = (bf16[800,128]{1,0:T(8,128)(2,1)S(1)}, bf16[800,128]{1,0:T(8,128)(2,1)S(1)}, u32[]{:S(2)}, u32[]{:S(2)}) collective-permute-start(bf16[800,128]{1,0:T(8,128)(2,1)S(1)} %get-tuple-element.14.refs_3_), channel_id=1, source_target_pairs={{0,6},{1,7},{2,0},{3,1},{4,2},{5,3},{6,4},{7,5},{8,14},{9,15},{10,... | collective-permute-start | bytes 614408 | tf_op jit(solution)/shard_map/ppermute | solution.py:246
  29.0 16.4 %collective-permute-start = (bf16[800,128]{1,0:T(8,128)(2,1)S(1)}, bf16[800,128]{1,0:T(8,128)(2,1)S(1)}, u32[]{:S(2)}, u32[]{:S(2)}) collective-permute-start(bf16[800,128]{1,0:T(8,128)(2,1)S(1)} %get-tuple-element.15.refs_2_), channel_id=1, source_target_pairs={{0,1},{1,0},{2,3},{3,2},{4,5},{5,4},{6,7},{7,6},{8,9},{9,8},{10,11... | collective-permute-start | bytes 614408 | tf_op jit(solution)/shard_map/ppermute | solution.py:246
  30.5 16.3 %collective-permute-start.1 = (bf16[800,128]{1,0:T(8,128)(2,1)S(1)}, bf16[800,128]{1,0:T(8,128)(2,1)S(1)}, u32[]{:S(2)}, u32[]{:S(2)}) collective-permute-start(bf16[800,128]{1,0:T(8,128)(2,1)S(1)} %get-tuple-element.14.refs_3_), channel_id=1, source_target_pairs={{0,1},{1,0},{2,3},{3,2},{4,5},{5,4},{6,7},{7,6},{8,9},{9,8},{10,11... | collective-permute-start | bytes 614408 | tf_op jit(solution)/shard_map/ppermute | solution.py:246
  30.5 33.2 %collective-permute-start.4 = (bf16[800,128]{1,0:T(8,128)(2,1)S(1)}, bf16[800,128]{1,0:T(8,128)(2,1)S(1)}, u32[]{:S(2)}, u32[]{:S(2)}) collective-permute-start(bf16[800,128]{1,0:T(8,128)(2,1)S(1)} %collective-permute-done.2.refs_6_), channel_id=1, source_target_pairs={{0,1},{1,0},{2,3},{3,2},{4,5},{5,4},{6,7},{7,6},{8,9},{9,8},{10,11... | collective-permute-start | bytes 614408 | tf_op jit(solution)/shard_map/ppermute | solution.py:246
  43.1 24.4 %collective-permute-start.5 = (bf16[800,128]{1,0:T(8,128)(2,1)S(1)}, bf16[800,128]{1,0:T(8,128)(2,1)S(1)}, u32[]{:S(2)}, u32[]{:S(2)}) collective-permute-start(bf16[800,128]{1,0:T(8,128)(2,1)S(1)} %collective-permute-done.3.refs_7_), channel_id=1, source_target_pairs={{0,1},{1,0},{2,3},{3,2},{4,5},{5,4},{6,7},{7,6},{8,9},{9,8},{10,11... | collective-permute-start | bytes 614408 | tf_op jit(solution)/shard_map/ppermute | solution.py:246
  46.1 22.2 %collective-permute-start.8 = (bf16[800,128]{1,0:T(8,128)(2,1)S(1)}, bf16[800,128]{1,0:T(8,128)(2,1)S(1)}, u32[]{:S(2)}, u32[]{:S(2)}) collective-permute-start(bf16[800,128]{1,0:T(8,128)(2,1)S(1)} %collective-permute-done.6.refs_10_), channel_id=1, source_target_pairs={{0,1},{1,0},{2,3},{3,2},{4,5},{5,4},{6,7},{7,6},{8,9},{9,8},{10,11... | collective-permute-start | bytes 614408 | tf_op jit(solution)/shard_map/ppermute | solution.py:246
  47.5 32.2 %collective-permute-start.17 = (bf16[1600,128]{1,0:T(8,128)(2,1)S(1)}, bf16[1600,128]{1,0:T(8,128)(2,1)S(1)}, u32[]{:S(2)}, u32[]{:S(2)}) collective-permute-start(bf16[1600,128]{1,0:T(8,128)(2,1)S(1)} %slice_bitcast_fusion.refs_2_), channel_id=1, source_target_pairs={{0,6},{1,3},{2,0},{3,5},{4,2},{5,7},{6,4},{7,1},{8,14},{9,11},{10,... | collective-permute-start | bytes 1228808 | tf_op jit(solution)/shard_map/ppermute | solution.py:262
  64.5 9.4 %collective-permute-start.10 = (bf16[800,128]{1,0:T(8,128)(2,1)S(1)}, bf16[800,128]{1,0:T(8,128)(2,1)S(1)}, u32[]{:S(2)}, u32[]{:S(2)}) collective-permute-start(bf16[800,128]{1,0:T(8,128)(2,1)S(1)} %collective-permute-done.2.refs_6_), channel_id=1, source_target_pairs={{0,2},{1,3},{2,4},{3,5},{4,6},{5,7},{6,0},{7,1},{8,10},{9,11},{10,... | collective-permute-start | bytes 614408 | tf_op jit(solution)/shard_map/ppermute | solution.py:246
  64.5 17.0 %collective-permute-start.19 = (bf16[1600,128]{1,0:T(8,128)(2,1)S(1)}, bf16[1600,128]{1,0:T(8,128)(2,1)S(1)}, u32[]{:S(2)}, u32[]{:S(2)}) collective-permute-start(bf16[1600,128]{1,0:T(8,128)(2,1)S(1)} %collective-permute-done.15.refs_4_), channel_id=1, source_target_pairs={{0,2},{1,7},{2,4},{3,1},{4,6},{5,3},{6,0},{7,5},{8,10},{9,15},{10,... | collective-permute-start | bytes 1228808 | tf_op jit(solution)/shard_map/ppermute | solution.py:262
  69.0 9.0 %collective-permute-start.11 = (bf16[800,128]{1,0:T(8,128)(2,1)S(1)}, bf16[800,128]{1,0:T(8,128)(2,1)}, u32[]{:S(2)}, u32[]{:S(2)}) collective-permute-start(bf16[800,128]{1,0:T(8,128)(2,1)S(1)} %collective-permute-done.7.refs_11_), channel_id=1, source_target_pairs={{0,6},{1,7},{2,0},{3,1},{4,2},{5,3},{6,4},{7,5},{8,14},{9,15},{10,... | collective-permute-start | bytes 614408 | tf_op jit(solution)/shard_map/ppermute | solution.py:246
  75.3 26.8 %collective-permute-start.14 = (bf16[1600,128]{1,0:T(8,128)(2,1)S(1)}, bf16[1600,128]{1,0:T(8,128)(2,1)S(1)}, u32[]{:S(2)}, u32[]{:S(2)}) collective-permute-start(bf16[1600,128]{1,0:T(8,128)(2,1)S(1)} %slice_bitcast_fusion.refs_2_), channel_id=1, source_target_pairs={{0,1},{1,0},{2,3},{3,2},{4,5},{5,4},{6,7},{7,6},{8,9},{9,8},{10,11... | collective-permute-start | bytes 1228808 | tf_op jit(solution)/shard_map/ppermute | solution.py:246
  77.9 24.2 %collective-permute-start.16 = (bf16[1600,128]{1,0:T(8,128)(2,1)S(1)}, bf16[1600,128]{1,0:T(8,128)(2,1)S(1)}, u32[]{:S(2)}, u32[]{:S(2)}) collective-permute-start(bf16[1600,128]{1,0:T(8,128)(2,1)S(1)} %collective-permute-done.15.refs_4_), channel_id=1, source_target_pairs={{0,1},{1,0},{2,3},{3,2},{4,5},{5,4},{6,7},{7,6},{8,9},{9,8},{10,11... | collective-permute-start | bytes 1228808 | tf_op jit(solution)/shard_map/ppermute | solution.py:246
  79.7 22.4 %collective-permute-start.18 = (bf16[1600,128]{1,0:T(8,128)(2,1)S(1)}, bf16[1600,128]{1,0:T(8,128)(2,1)S(1)}, u32[]{:S(2)}, u32[]{:S(2)}) collective-permute-start(bf16[1600,128]{1,0:T(8,128)(2,1)S(1)} %collective-permute-done.17.refs_6_), channel_id=1, source_target_pairs={{0,1},{1,0},{2,3},{3,2},{4,5},{5,4},{6,7},{7,6},{8,9},{9,8},{10,11... | collective-permute-start | bytes 1228808 | tf_op jit(solution)/shard_map/ppermute | solution.py:246
  80.4 16.3 %collective-permute-start.13 = (bf16[800,128]{1,0:T(8,128)(2,1)}, bf16[800,128]{1,0:T(8,128)(2,1)}, u32[]{:S(2)}, u32[]{:S(2)}) collective-permute-start(bf16[800,128]{1,0:T(8,128)(2,1)} %collective-permute-done.11.refs_4_), channel_id=1, source_target_pairs={{0,1},{1,0},{2,3},{3,2},{4,5},{5,4},{6,7},{7,6},{8,9},{9,8},{10,11... | collective-permute-start | bytes 614408 | tf_op jit(solution)/shard_map/ppermute | solution.py:246
  81.4 27.5 %collective-permute-start.20 = (bf16[1600,128]{1,0:T(8,128)(2,1)S(1)}, bf16[1600,128]{1,0:T(8,128)(2,1)S(1)}, u32[]{:S(2)}, u32[]{:S(2)}) collective-permute-start(bf16[1600,128]{1,0:T(8,128)(2,1)S(1)} %collective-permute-done.19.refs_2_), channel_id=1, source_target_pairs={{0,1},{1,0},{2,3},{3,2},{4,5},{5,4},{6,7},{7,6},{8,9},{9,8},{10,11... | collective-permute-start | bytes 1228808 | tf_op jit(solution)/shard_map/ppermute | solution.py:246
  140.8 23.0 %all-to-all-start.2 = ((bf16[16,320,128]{2,1,0:T(8,128)(2,1)}), bf16[16,320,128]{2,1,0:T(8,128)(2,1)S(1)}, u32[]{:S(2)}, u32[]{:S(2)}) async-start(bf16[16,320,128]{2,1,0:T(8,128)(2,1)} %bitcast.40), calls=%async_computation.2 | async-start | bytes 2621440 | tf_op jit(solution)/shard_map/all_to_all | solution.py:328
  163.7 36.3 %all-to-all-start.1 = ((bf16[32,160,128]{2,1,0:T(8,128)(2,1)}), bf16[32,160,128]{2,1,0:T(8,128)(2,1)S(1)}, u32[]{:S(2)}, u32[]{:S(2)}) async-start(bf16[32,160,128]{2,1,0:T(8,128)(2,1)} %shard_map.74), calls=%async_computation.1 | async-start | bytes 2621440 | tf_op jit(solution)/shard_map/all_to_all | solution.py:364
  170.4 15.7 %collective-permute-start.21 = (bf16[320,128]{1,0:T(8,128)(2,1)S(1)}, bf16[320,128]{1,0:T(8,128)(2,1)S(1)}, u32[]{:S(2)}, u32[]{:S(2)}) collective-permute-start(bf16[320,128]{1,0:T(8,128)(2,1)S(1)} %shard_map.75.here), channel_id=1, source_target_pairs={{0,32},{1,33},{2,34},{3,35},{4,36},{5,37},{6,38},{7,39},{8,40},{9,... | collective-permute-start | bytes 245768 | tf_op jit(solution)/shard_map/ppermute | solution.py:323
  194.1 8.6 %collective-permute-start.25 = (bf16[1280,128]{1,0:T(8,128)(2,1)S(1)}, bf16[1280,128]{1,0:T(8,128)(2,1)S(1)}, u32[]{:S(2)}, u32[]{:S(2)}) collective-permute-start(bf16[1280,128]{1,0:T(8,128)(2,1)S(1)} %shard_map.77.refs_0_), channel_id=1, source_target_pairs={{0,64},{1,9},{2,66},{3,11},{4,68},{5,13},{6,70},{7,15},{8,72},{9,1... | collective-permute-start | bytes 983048 | tf_op jit(solution)/shard_map/ppermute | solution.py:323
  197.5 9.6 %collective-permute-start.27 = (bf16[1280,128]{1,0:T(8,128)(2,1)S(1)}, bf16[1280,128]{1,0:T(8,128)(2,1)S(1)}, u32[]{:S(2)}, u32[]{:S(2)}) collective-permute-start(bf16[1280,128]{1,0:T(8,128)(2,1)S(1)} %shard_map.77.refs_0_), channel_id=1, source_target_pairs={{0,128},{1,17},{2,130},{3,19},{4,132},{5,21},{6,134},{7,23},{8,136... | collective-permute-start | bytes 983048 | tf_op jit(solution)/shard_map/ppermute | solution.py:323
  (30 other events, 94.2 us)

commit v3 on v2

--- a/solution.py
+++ b/solution.py
@@ -64,12 +64,9 @@
     def kernel(me, wanted, *refs):
         extra = 4 if first and late else 1
         refs, (x, g, m_buf, want, fetched, loaded, stored, *bufs) = refs[: -7 - extra], refs[-7 - extra :]
-        full = half = None
-        if first:
+        if first and late:
             full, *refs = refs
-        if late or not first:
-            half, *refs = refs
-        moment, *refs = refs
+        half, moment, *refs = refs
         count = 2 * len(ups) * (2 - step)
         blocks, outs = refs[:count], refs[count:]
         units = wanted.shape[1]
@@ -83,22 +80,16 @@
                 moves += [(blocks[2 * i], x.at[:TOP, lanes]), (blocks[2 * i + 1], x.at[TOP:, lanes])]
             fetches.append([pltpu.make_async_copy(*m, fetched.at[i, k]) for k, m in enumerate(moves)])
         loads = []
-        if first:
-            w_buf = bufs[1 if late else 0]
+        if first and late:
+            w_buf = bufs[1]
             loads.append(pltpu.make_async_copy(full, w_buf, loaded.at[0]))
         if not late:
             loads.append(pltpu.make_async_copy(moment, m_buf, loaded.at[1]))
-        if first and not late:
-            loads[0].start()
         for fetch in fetches:
             for copy in fetch:
                 copy.start()
-        for load in loads[first and not late :]:
+        for load in loads:
             load.start()
-        if first and not late:
-            loads.pop(0).wait()
-            half = outs[1]
-            half[...] = w_buf[...].astype(jnp.bfloat16)
         for fetch in fetches:
             for copy in fetch:
                 copy.wait()
@@ -197,9 +188,9 @@
     units, tokens = wanted.shape[1], 2 * LANES * len(ups)
     whole, half = ((units, D), jnp.float32), ((units, D), jnp.bfloat16)
     lines = (units // UNITS * LINES, LANES), jnp.bfloat16
-    outs = [[[whole], [lines]], [[whole, half], [lines, half, half]]][first][late]
+    outs = [whole] if not late else [lines, half, half] if first else [lines]
     small = (8, LANES), jnp.float32
-    bufs = [lines if late else whole if first else small]
+    bufs = [lines if late else small]
     if first and late:
         bufs = [lines, whole, half, half]
     args = [kept(w) if w.dtype == jnp.float32 else w for w in weights]
@@ -228,6 +219,10 @@
     )(me, kept(wanted), *args, *blocks)
 
 
+def half_kernel(weight, out):
+    out[...] = weight[...].astype(jnp.bfloat16)
+
+
 def gate_kernel(me, out):
     out[0] = me[0]
 
@@ -353,7 +348,8 @@
     near2, far2 = gather_whole(second)
 
     ready = gate(me)
-    moment, old = local_step(ready, wanted, [weight], moment, near, 0, (0, 3, 1))
+    old = small(half_kernel, [weight], (units, D))
+    (moment,) = local_step(ready, wanted, [old], moment, near, 0, (0, 3, 1))
     weight_lines, weight, moment = local_step(me, wanted, [weight, old], moment, far, 0, (2,))
     parts = weight_mean(weight_lines)
 

time: 213 us -> 205 us (0.962)
  local copies, waits for them, and re-layouts: 19.4 us -> 14.1 us
    unnamed x48 -> x50, local copies, waits for them, and re-layouts: 17.2 us -> 11.8 us
where the time goes in v3:
time: 205 us; the launch traced here: 202 us
  waiting for transfers between devices  66.9 us (33%)
  starting transfers between devices  63.7 us (31%)
  Pallas kernels  28.8 us (14%)
  blocking collectives  27.2 us (13%)
  local copies, waits for them, and re-layouts  14.1 us (7%)
    ppermute x18, waiting for transfers between devices, shard_permute(): return lax.ppermute(v, 'shard', rotated(up, cores))  27.9 us
    all_to_all x1, blocking collectives, body(): got = lax.all_to_all(moment_lines.reshape(replicas, -1, LANES), 'rep', 0, 0)  27.2 us
    ppermute x3, starting transfers between devices, passed(): return lax.ppermute(v, 'shard', pairs)  25.4 us
    ppermute x7, waiting for transfers between devices, replica_permute(): return lax.ppermute(v, ('rep', 'shard'), pairs)  22.7 us
    pallas_call x4, Pallas kernels, local_step(): pl.pallas_call(step_kernel(step, ups, late), out_shape=tuple(((pltpu.HBM...  21.1 us
    ppermute x18, starting transfers between devices, shard_permute(): return lax.ppermute(v, 'shard', rotated(up, cores))  17.5 us
    all_to_all x1, waiting for transfers between devices, weight_mean(): lax.all_to_all(lines.reshape(16, -1, LANES), 'rep', 0, 0, axis_index_grou...  16.4 us
    unnamed x50, local copies, waits for them, and re-layouts  11.8 us
  transfers between devices with their start and end apart: 30, of which 11 were waited for; matrix products, arithmetic and copies ran while one was open for 1% of the time, Pallas kernels for 11%

profile of v3, /device:TPU:8, one launch (start us, length us, event | category | flops | bytes accessed | tf_op | source)
XLA Modules:
  0.0 201.8 jit_solution(16513246862461340349)
XLA Ops:
  1.7 3.3 %collective-permute-start.2 = (bf16[800,128]{1,0:T(8,128)(2,1)S(1)}, bf16[800,128]{1,0:T(8,128)(2,1)S(1)}, u32[]{:S(2)}, u32[]{:S(2)}) collective-permute-start(bf16[800,128]{1,0:T(8,128)(2,1)S(1)} %get-tuple-element.11.refs_2_), channel_id=1, source_target_pairs={{0,2},{1,3},{2,4},{3,5},{4,6},{5,7},{6,0},{7,1},{8,10},{9,11},{10,... | collective-permute-start | bytes 614408 | tf_op jit(solution)/shard_map/ppermute | solution.py:241
  5.0 3.1 %collective-permute-start.6 = (bf16[800,128]{1,0:T(8,128)(2,1)S(1)}, bf16[800,128]{1,0:T(8,128)(2,1)S(1)}, u32[]{:S(2)}, u32[]{:S(2)}) collective-permute-start(bf16[800,128]{1,0:T(8,128)(2,1)S(1)} %get-tuple-element.11.refs_2_), channel_id=1, source_target_pairs={{0,6},{1,7},{2,0},{3,1},{4,2},{5,3},{6,4},{7,5},{8,14},{9,15},{10,... | collective-permute-start | bytes 614408 | tf_op jit(solution)/shard_map/ppermute | solution.py:241
  10.6 10.4 %collective-permute-done.3.refs_7_ = bf16[800,128]{1,0:T(8,128)(2,1)S(1)} collective-permute-done((bf16[800,128]{1,0:T(8,128)(2,1)S(1)}, bf16[800,128]{1,0:T(8,128)(2,1)S(1)}, u32[]{:S(2)}, u32[]{:S(2)}) %collective-permute-start.3) | collective-permute-done | bytes 204832 | tf_op jit(solution)/shard_map/ppermute | solution.py:241
  20.9 6.0 %collective-permute-start.15 = (bf16[1600,128]{1,0:T(8,128)(2,1)S(1)}, bf16[1600,128]{1,0:T(8,128)(2,1)S(1)}, u32[]{:S(2)}, u32[]{:S(2)}) collective-permute-start(bf16[1600,128]{1,0:T(8,128)(2,1)S(1)} %slice_bitcast_fusion.refs_2_), channel_id=1, source_target_pairs={{0,2},{1,7},{2,4},{3,1},{4,6},{5,3},{6,0},{7,5},{8,10},{9,15},{10,... | collective-permute-start | bytes 1228808 | tf_op jit(solution)/shard_map/ppermute | solution.py:257
  26.9 2.1 %collective-permute-start.7 = (bf16[800,128]{1,0:T(8,128)(2,1)S(1)}, bf16[800,128]{1,0:T(8,128)(2,1)S(1)}, u32[]{:S(2)}, u32[]{:S(2)}) collective-permute-start(bf16[800,128]{1,0:T(8,128)(2,1)S(1)} %get-tuple-element.10.refs_3_), channel_id=1, source_target_pairs={{0,6},{1,7},{2,0},{3,1},{4,2},{5,3},{6,4},{7,5},{8,14},{9,15},{10,... | collective-permute-start | bytes 614408 | tf_op jit(solution)/shard_map/ppermute | solution.py:241
  31.0 12.1 %collective-permute-done.7.refs_11_ = bf16[800,128]{1,0:T(8,128)(2,1)S(1)} collective-permute-done((bf16[800,128]{1,0:T(8,128)(2,1)S(1)}, bf16[800,128]{1,0:T(8,128)(2,1)S(1)}, u32[]{:S(2)}, u32[]{:S(2)}) %collective-permute-start.7) | collective-permute-done | bytes 204832 | tf_op jit(solution)/shard_map/ppermute | solution.py:241
  47.5 16.3 %collective-permute-start.17 = (bf16[1600,128]{1,0:T(8,128)(2,1)S(1)}, bf16[1600,128]{1,0:T(8,128)(2,1)S(1)}, u32[]{:S(2)}, u32[]{:S(2)}) collective-permute-start(bf16[1600,128]{1,0:T(8,128)(2,1)S(1)} %slice_bitcast_fusion.refs_2_), channel_id=1, source_target_pairs={{0,6},{1,3},{2,0},{3,5},{4,2},{5,7},{6,4},{7,1},{8,14},{9,11},{10,... | collective-permute-start | bytes 1228808 | tf_op jit(solution)/shard_map/ppermute | solution.py:257
  64.5 3.1 %collective-permute-start.19 = (bf16[1600,128]{1,0:T(8,128)(2,1)S(1)}, bf16[1600,128]{1,0:T(8,128)(2,1)S(1)}, u32[]{:S(2)}, u32[]{:S(2)}) collective-permute-start(bf16[1600,128]{1,0:T(8,128)(2,1)S(1)} %collective-permute-done.15.refs_4_), channel_id=1, source_target_pairs={{0,2},{1,7},{2,4},{3,1},{4,6},{5,3},{6,0},{7,5},{8,10},{9,15},{10,... | collective-permute-start | bytes 1228808 | tf_op jit(solution)/shard_map/ppermute | solution.py:257
  70.7 3.2 %collective-permute-done.10.refs_3_ = bf16[800,128]{1,0:T(8,128)(2,1)S(1)} collective-permute-done((bf16[800,128]{1,0:T(8,128)(2,1)S(1)}, bf16[800,128]{1,0:T(8,128)(2,1)S(1)}, u32[]{:S(2)}, u32[]{:S(2)}) %collective-permute-start.10) | collective-permute-done | bytes 204832 | tf_op jit(solution)/shard_map/ppermute | solution.py:241
  75.8 2.2 %collective-permute-done.11.refs_4_ = bf16[800,128]{1,0:T(8,128)(2,1)} collective-permute-done((bf16[800,128]{1,0:T(8,128)(2,1)S(1)}, bf16[800,128]{1,0:T(8,128)(2,1)}, u32[]{:S(2)}, u32[]{:S(2)}) %collective-permute-start.11) | collective-permute-done | bytes 204832 | tf_op jit(solution)/shard_map/ppermute | solution.py:241
  84.7 6.1 %shard_map.71.refs_2_ = f32[400,1600]{1,0:T(8,128)S(1)} custom-call(s32[1]{0:T(128)} %shard_map.70.me, bf16[2,400,1024]{2,1,0:T(8,128)(2,1)} %bitcast.32, bf16[400,1600]{1,0:T(8,128)(2,1)S(1)} %shard_map.69.refs_0_.refs_1_, f32[400,1600]{1,0:T(8,128)} %bitcast.37, bf16[800,128]{1,0:T(8,128)(2,1)S(1)} %get-tuple-element.11.refs_2_, ...), custom_call_target="tpu_custom_call" | custom-call | flops 1966080000 | bytes 5120000 | tf_op jit(solution)/shard_map/pallas_call | solution.py:200
  90.9 5.4 %shard_map.72 = (bf16[5120,128]{1,0:T(8,128)(2,1)}, bf16[400,1600]{1,0:T(8,128)(2,1)}, bf16[400,1600]{1,0:T(8,128)(2,1)}) custom-call(s32[1]{0:T(128)} %bitcast.1.me, bf16[2,400,1024]{2,1,0:T(8,128)(2,1)} %bitcast.33, f32[400,1600]{1,0:T(8,128)} %bitcast.30, bf16[400,1600]{1,0:T(8,128)(2,1)S(1)} %shard_map.69.refs_0_.refs_1_, ...), custom_call_target="tpu_custom_call" | custom-call | flops 655360000 | bytes 5120000 | tf_op jit(solution)/shard_map/pallas_call | solution.py:200
  97.6 5.5 %shard_map.73.refs_1_ = f32[400,1600]{1,0:T(8,128)S(1)} custom-call(s32[1]{0:T(128)} %bitcast.1.me, bf16[2,400,1024]{2,1,0:T(8,128)(2,1)} %bitcast.34, bf16[400,1600]{1,0:T(8,128)(2,1)S(1)} %copy-done.1, bf16[400,1600]{1,0:T(8,128)(2,1)} %get-tuple-element.7.refs_1_, bf16[1600,128]{1,0:T(8,128)(2,1)S(1)} %slice_bitcast_fusion.refs_2_, ...), custom_call_target="tpu_custom_call" | custom-call | flops 1966080000 | bytes 5120000 | tf_op jit(solution)/shard_map/pallas_call | solution.py:200
  103.2 4.1 %shard_map.74.moment = bf16[5120,128]{1,0:T(8,128)(2,1)} custom-call(s32[1]{0:T(128)} %bitcast.1.me, bf16[2,400,1024]{2,1,0:T(8,128)(2,1)} %bitcast.35, bf16[400,1600]{1,0:T(8,128)(2,1)S(1)} %copy-done.1, f32[400,1600]{1,0:T(8,128)S(1)} %shard_map.73.refs_1_, bf16[1600,128]{1,0:T(8,128)(2,1)S(1)} %collective-permute-done.19.refs_2_, ...), custom_call_target="tpu_custom_call" | custom-call | flops 655360000 | bytes 5120000 | tf_op jit(solution)/shard_map/pallas_call | solution.py:200
  107.2 27.2 %all_to_all.15.got = bf16[32,160,128]{2,1,0:T(8,128)(2,1)S(1)} all-to-all(bf16[32,160,128]{2,1,0:T(8,128)(2,1)} %bitcast.36), channel_id=1, replica_groups=mesh['rep'=32,'shard'=8] {'rep'}, dimensions={0} | all-to-all | bytes 2621440 | tf_op jit(solution)/shard_map/all_to_all | solution.py:358
  134.4 4.6 %all-to-all-start.2 = ((bf16[16,320,128]{2,1,0:T(8,128)(2,1)}), bf16[16,320,128]{2,1,0:T(8,128)(2,1)S(1)}, u32[]{:S(2)}, u32[]{:S(2)}) async-start(bf16[16,320,128]{2,1,0:T(8,128)(2,1)} %bitcast.40), calls=%async_computation.2 | async-start | bytes 2621440 | tf_op jit(solution)/shard_map/all_to_all | solution.py:323
  140.3 16.4 %all-to-all-done.2.got = bf16[16,320,128]{2,1,0:T(8,128)(2,1)S(1)} async-done(((bf16[16,320,128]{2,1,0:T(8,128)(2,1)}), bf16[16,320,128]{2,1,0:T(8,128)(2,1)S(1)}, u32[]{:S(2)}, u32[]{:S(2)}) %all-to-all-start.2) | async-done | bytes 1310752 | tf_op jit(solution)/shard_map/all_to_all | solution.py:323
  156.7 5.3 %all-to-all-start.1 = ((bf16[32,160,128]{2,1,0:T(8,128)(2,1)}), bf16[32,160,128]{2,1,0:T(8,128)(2,1)S(1)}, u32[]{:S(2)}, u32[]{:S(2)}) async-start(bf16[32,160,128]{2,1,0:T(8,128)(2,1)} %shard_map.75), calls=%async_computation.1 | async-start | bytes 2621440 | tf_op jit(solution)/shard_map/all_to_all | solution.py:360
  163.8 14.4 %collective-permute-done.21.there = bf16[320,128]{1,0:T(8,128)(2,1)S(1)} collective-permute-done((bf16[320,128]{1,0:T(8,128)(2,1)S(1)}, bf16[320,128]{1,0:T(8,128)(2,1)S(1)}, u32[]{:S(2)}, u32[]{:S(2)}) %collective-permute-start.21) | collective-permute-done | bytes 81952 | tf_op jit(solution)/shard_map/ppermute | solution.py:318
  180.3 2.1 %collective-permute-start.24 = (bf16[320,128]{1,0:T(8,128)(2,1)S(1)}, bf16[320,128]{1,0:T(8,128)(2,1)S(1)}, u32[]{:S(2)}, u32[]{:S(2)}) collective-permute-start(bf16[320,128]{1,0:T(8,128)(2,1)S(1)} %shard_map.77.refs_0_), channel_id=1, source_target_pairs={{0,16},{1,129},{2,18},{3,131},{4,20},{5,133},{6,22},{7,135},{8,24}... | collective-permute-start | bytes 245768 | tf_op jit(solution)/shard_map/ppermute | solution.py:318
  184.2 2.1 %collective-permute-done.24.refs_3_ = bf16[320,128]{1,0:T(8,128)(2,1)S(1)} collective-permute-done((bf16[320,128]{1,0:T(8,128)(2,1)S(1)}, bf16[320,128]{1,0:T(8,128)(2,1)S(1)}, u32[]{:S(2)}, u32[]{:S(2)}) %collective-permute-start.24) | collective-permute-done | bytes 81952 | tf_op jit(solution)/shard_map/ppermute | solution.py:318
  192.1 2.7 %blended.1 = f32[400,1600]{1,0:T(8,128)} custom-call(f32[400,1]{1,0:T(8,128)S(1)} %copy.7.blend, bf16[5120,128]{1,0:T(8,128)(2,1)S(1)} %bitcast.28, bf16[5120,128]{1,0:T(8,128)(2,1)} %shard_map.74.moment), custom_call_target="tpu_custom_call" | custom-call | tf_op jit(solution)/shard_map/blended/pallas_call | solution.py:362
  195.0 4.2 %collective-permute-done.27.refs_3_ = bf16[1280,128]{1,0:T(8,128)(2,1)S(1)} collective-permute-done((bf16[1280,128]{1,0:T(8,128)(2,1)S(1)}, bf16[1280,128]{1,0:T(8,128)(2,1)S(1)}, u32[]{:S(2)}, u32[]{:S(2)}) %collective-permute-start.27) | collective-permute-done | bytes 327712 | tf_op jit(solution)/shard_map/ppermute | solution.py:318
  199.2 2.4 %averaged.1 = f32[400,1600]{1,0:T(8,128)} custom-call(s32[1]{0:T(128)} %shard_map.68.rep, s32[1]{0:T(128)} %bitcast.1.me, bf16[5120,128]{1,0:T(8,128)(2,1)S(1)} %bitcast.29, bf16[1280,128]{1,0:T(8,128)(2,1)S(1)} %shard_map.78.refs_0_, bf16[1280,128]{1,0:T(8,128)(2,1)S(1)} %collective-permute-done.25.refs_1_, ...), custom_call_target="tpu_custom_call" | custom-call | tf_op jit(solution)/shard_map/averaged/pallas_call | solution.py:376
  (103 shorter events, 36.5 us)
Async XLA Ops:
  1.7 28.8 %collective-permute-start.2 = (bf16[800,128]{1,0:T(8,128)(2,1)S(1)}, bf16[800,128]{1,0:T(8,128)(2,1)S(1)}, u32[]{:S(2)}, u32[]{:S(2)}) collective-permute-start(bf16[800,128]{1,0:T(8,128)(2,1)S(1)} %get-tuple-element.11.refs_2_), channel_id=1, source_target_pairs={{0,2},{1,3},{2,4},{3,5},{4,6},{5,7},{6,0},{7,1},{8,10},{9,11},{10,... | collective-permute-start | bytes 614408 | tf_op jit(solution)/shard_map/ppermute | solution.py:241
  5.0 15.9 %collective-permute-start.6 = (bf16[800,128]{1,0:T(8,128)(2,1)S(1)}, bf16[800,128]{1,0:T(8,128)(2,1)S(1)}, u32[]{:S(2)}, u32[]{:S(2)}) collective-permute-start(bf16[800,128]{1,0:T(8,128)(2,1)S(1)} %get-tuple-element.11.refs_2_), channel_id=1, source_target_pairs={{0,6},{1,7},{2,0},{3,1},{4,2},{5,3},{6,4},{7,5},{8,14},{9,15},{10,... | collective-permute-start | bytes 614408 | tf_op jit(solution)/shard_map/ppermute | solution.py:241
  8.2 12.8 %collective-permute-start.3 = (bf16[800,128]{1,0:T(8,128)(2,1)S(1)}, bf16[800,128]{1,0:T(8,128)(2,1)S(1)}, u32[]{:S(2)}, u32[]{:S(2)}) collective-permute-start(bf16[800,128]{1,0:T(8,128)(2,1)S(1)} %get-tuple-element.10.refs_3_), channel_id=1, source_target_pairs={{0,2},{1,3},{2,4},{3,5},{4,6},{5,7},{6,0},{7,1},{8,10},{9,11},{10,... | collective-permute-start | bytes 614408 | tf_op jit(solution)/shard_map/ppermute | solution.py:241
  20.9 43.5 %collective-permute-start.15 = (bf16[1600,128]{1,0:T(8,128)(2,1)S(1)}, bf16[1600,128]{1,0:T(8,128)(2,1)S(1)}, u32[]{:S(2)}, u32[]{:S(2)}) collective-permute-start(bf16[1600,128]{1,0:T(8,128)(2,1)S(1)} %slice_bitcast_fusion.refs_2_), channel_id=1, source_target_pairs={{0,2},{1,7},{2,4},{3,1},{4,6},{5,3},{6,0},{7,5},{8,10},{9,15},{10,... | collective-permute-start | bytes 1228808 | tf_op jit(solution)/shard_map/ppermute | solution.py:257
  26.9 16.2 %collective-permute-start.7 = (bf16[800,128]{1,0:T(8,128)(2,1)S(1)}, bf16[800,128]{1,0:T(8,128)(2,1)S(1)}, u32[]{:S(2)}, u32[]{:S(2)}) collective-permute-start(bf16[800,128]{1,0:T(8,128)(2,1)S(1)} %get-tuple-element.10.refs_3_), channel_id=1, source_target_pairs={{0,6},{1,7},{2,0},{3,1},{4,2},{5,3},{6,4},{7,5},{8,14},{9,15},{10,... | collective-permute-start | bytes 614408 | tf_op jit(solution)/shard_map/ppermute | solution.py:241
  29.0 16.4 %collective-permute-start = (bf16[800,128]{1,0:T(8,128)(2,1)S(1)}, bf16[800,128]{1,0:T(8,128)(2,1)S(1)}, u32[]{:S(2)}, u32[]{:S(2)}) collective-permute-start(bf16[800,128]{1,0:T(8,128)(2,1)S(1)} %get-tuple-element.11.refs_2_), channel_id=1, source_target_pairs={{0,1},{1,0},{2,3},{3,2},{4,5},{5,4},{6,7},{7,6},{8,9},{9,8},{10,11... | collective-permute-start | bytes 614408 | tf_op jit(solution)/shard_map/ppermute | solution.py:241
  30.5 16.3 %collective-permute-start.1 = (bf16[800,128]{1,0:T(8,128)(2,1)S(1)}, bf16[800,128]{1,0:T(8,128)(2,1)S(1)}, u32[]{:S(2)}, u32[]{:S(2)}) collective-permute-start(bf16[800,128]{1,0:T(8,128)(2,1)S(1)} %get-tuple-element.10.refs_3_), channel_id=1, source_target_pairs={{0,1},{1,0},{2,3},{3,2},{4,5},{5,4},{6,7},{7,6},{8,9},{9,8},{10,11... | collective-permute-start | bytes 614408 | tf_op jit(solution)/shard_map/ppermute | solution.py:241
  30.5 33.2 %collective-permute-start.4 = (bf16[800,128]{1,0:T(8,128)(2,1)S(1)}, bf16[800,128]{1,0:T(8,128)(2,1)S(1)}, u32[]{:S(2)}, u32[]{:S(2)}) collective-permute-start(bf16[800,128]{1,0:T(8,128)(2,1)S(1)} %collective-permute-done.2.refs_6_), channel_id=1, source_target_pairs={{0,1},{1,0},{2,3},{3,2},{4,5},{5,4},{6,7},{7,6},{8,9},{9,8},{10,11... | collective-permute-start | bytes 614408 | tf_op jit(solution)/shard_map/ppermute | solution.py:241
  43.1 24.4 %collective-permute-start.5 = (bf16[800,128]{1,0:T(8,128)(2,1)S(1)}, bf16[800,128]{1,0:T(8,128)(2,1)S(1)}, u32[]{:S(2)}, u32[]{:S(2)}) collective-permute-start(bf16[800,128]{1,0:T(8,128)(2,1)S(1)} %collective-permute-done.3.refs_7_), channel_id=1, source_target_pairs={{0,1},{1,0},{2,3},{3,2},{4,5},{5,4},{6,7},{7,6},{8,9},{9,8},{10,11... | collective-permute-start | bytes 614408 | tf_op jit(solution)/shard_map/ppermute | solution.py:241
  46.1 22.2 %collective-permute-start.8 = (bf16[800,128]{1,0:T(8,128)(2,1)S(1)}, bf16[800,128]{1,0:T(8,128)(2,1)S(1)}, u32[]{:S(2)}, u32[]{:S(2)}) collective-permute-start(bf16[800,128]{1,0:T(8,128)(2,1)S(1)} %collective-permute-done.6.refs_10_), channel_id=1, source_target_pairs={{0,1},{1,0},{2,3},{3,2},{4,5},{5,4},{6,7},{7,6},{8,9},{9,8},{10,11... | collective-permute-start | bytes 614408 | tf_op jit(solution)/shard_map/ppermute | solution.py:241
  47.5 32.2 %collective-permute-start.17 = (bf16[1600,128]{1,0:T(8,128)(2,1)S(1)}, bf16[1600,128]{1,0:T(8,128)(2,1)S(1)}, u32[]{:S(2)}, u32[]{:S(2)}) collective-permute-start(bf16[1600,128]{1,0:T(8,128)(2,1)S(1)} %slice_bitcast_fusion.refs_2_), channel_id=1, source_target_pairs={{0,6},{1,3},{2,0},{3,5},{4,2},{5,7},{6,4},{7,1},{8,14},{9,11},{10,... | collective-permute-start | bytes 1228808 | tf_op jit(solution)/shard_map/ppermute | solution.py:257
  64.5 9.4 %collective-permute-start.10 = (bf16[800,128]{1,0:T(8,128)(2,1)S(1)}, bf16[800,128]{1,0:T(8,128)(2,1)S(1)}, u32[]{:S(2)}, u32[]{:S(2)}) collective-permute-start(bf16[800,128]{1,0:T(8,128)(2,1)S(1)} %collective-permute-done.2.refs_6_), channel_id=1, source_target_pairs={{0,2},{1,3},{2,4},{3,5},{4,6},{5,7},{6,0},{7,1},{8,10},{9,11},{10,... | collective-permute-start | bytes 614408 | tf_op jit(solution)/shard_map/ppermute | solution.py:241
  64.5 18.9 %collective-permute-start.19 = (bf16[1600,128]{1,0:T(8,128)(2,1)S(1)}, bf16[1600,128]{1,0:T(8,128)(2,1)S(1)}, u32[]{:S(2)}, u32[]{:S(2)}) collective-permute-start(bf16[1600,128]{1,0:T(8,128)(2,1)S(1)} %collective-permute-done.15.refs_4_), channel_id=1, source_target_pairs={{0,2},{1,7},{2,4},{3,1},{4,6},{5,3},{6,0},{7,5},{8,10},{9,15},{10,... | collective-permute-start | bytes 1228808 | tf_op jit(solution)/shard_map/ppermute | solution.py:257
  69.0 9.0 %collective-permute-start.11 = (bf16[800,128]{1,0:T(8,128)(2,1)S(1)}, bf16[800,128]{1,0:T(8,128)(2,1)}, u32[]{:S(2)}, u32[]{:S(2)}) collective-permute-start(bf16[800,128]{1,0:T(8,128)(2,1)S(1)} %collective-permute-done.7.refs_11_), channel_id=1, source_target_pairs={{0,6},{1,7},{2,0},{3,1},{4,2},{5,3},{6,4},{7,5},{8,14},{9,15},{10,... | collective-permute-start | bytes 614408 | tf_op jit(solution)/shard_map/ppermute | solution.py:241
  75.3 21.0 %collective-permute-start.14 = (bf16[1600,128]{1,0:T(8,128)(2,1)S(1)}, bf16[1600,128]{1,0:T(8,128)(2,1)S(1)}, u32[]{:S(2)}, u32[]{:S(2)}) collective-permute-start(bf16[1600,128]{1,0:T(8,128)(2,1)S(1)} %slice_bitcast_fusion.refs_2_), channel_id=1, source_target_pairs={{0,1},{1,0},{2,3},{3,2},{4,5},{5,4},{6,7},{7,6},{8,9},{9,8},{10,11... | collective-permute-start | bytes 1228808 | tf_op jit(solution)/shard_map/ppermute | solution.py:241
  77.9 18.4 %collective-permute-start.16 = (bf16[1600,128]{1,0:T(8,128)(2,1)S(1)}, bf16[1600,128]{1,0:T(8,128)(2,1)S(1)}, u32[]{:S(2)}, u32[]{:S(2)}) collective-permute-start(bf16[1600,128]{1,0:T(8,128)(2,1)S(1)} %collective-permute-done.15.refs_4_), channel_id=1, source_target_pairs={{0,1},{1,0},{2,3},{3,2},{4,5},{5,4},{6,7},{7,6},{8,9},{9,8},{10,11... | collective-permute-start | bytes 1228808 | tf_op jit(solution)/shard_map/ppermute | solution.py:241
  79.7 16.6 %collective-permute-start.18 = (bf16[1600,128]{1,0:T(8,128)(2,1)S(1)}, bf16[1600,128]{1,0:T(8,128)(2,1)S(1)}, u32[]{:S(2)}, u32[]{:S(2)}) collective-permute-start(bf16[1600,128]{1,0:T(8,128)(2,1)S(1)} %collective-permute-done.17.refs_6_), channel_id=1, source_target_pairs={{0,1},{1,0},{2,3},{3,2},{4,5},{5,4},{6,7},{7,6},{8,9},{9,8},{10,11... | collective-permute-start | bytes 1228808 | tf_op jit(solution)/shard_map/ppermute | solution.py:241
  80.4 10.5 %collective-permute-start.13 = (bf16[800,128]{1,0:T(8,128)(2,1)}, bf16[800,128]{1,0:T(8,128)(2,1)}, u32[]{:S(2)}, u32[]{:S(2)}) collective-permute-start(bf16[800,128]{1,0:T(8,128)(2,1)} %collective-permute-done.11.refs_4_), channel_id=1, source_target_pairs={{0,1},{1,0},{2,3},{3,2},{4,5},{5,4},{6,7},{7,6},{8,9},{9,8},{10,11... | collective-permute-start | bytes 614408 | tf_op jit(solution)/shard_map/ppermute | solution.py:241
  83.4 19.8 %collective-permute-start.20 = (bf16[1600,128]{1,0:T(8,128)(2,1)S(1)}, bf16[1600,128]{1,0:T(8,128)(2,1)S(1)}, u32[]{:S(2)}, u32[]{:S(2)}) collective-permute-start(bf16[1600,128]{1,0:T(8,128)(2,1)S(1)} %collective-permute-done.19.refs_2_), channel_id=1, source_target_pairs={{0,1},{1,0},{2,3},{3,2},{4,5},{5,4},{6,7},{7,6},{8,9},{9,8},{10,11... | collective-permute-start | bytes 1228808 | tf_op jit(solution)/shard_map/ppermute | solution.py:241
  134.4 22.3 %all-to-all-start.2 = ((bf16[16,320,128]{2,1,0:T(8,128)(2,1)}), bf16[16,320,128]{2,1,0:T(8,128)(2,1)S(1)}, u32[]{:S(2)}, u32[]{:S(2)}) async-start(bf16[16,320,128]{2,1,0:T(8,128)(2,1)} %bitcast.40), calls=%async_computation.2 | async-start | bytes 2621440 | tf_op jit(solution)/shard_map/all_to_all | solution.py:323
  156.7 35.4 %all-to-all-start.1 = ((bf16[32,160,128]{2,1,0:T(8,128)(2,1)}), bf16[32,160,128]{2,1,0:T(8,128)(2,1)S(1)}, u32[]{:S(2)}, u32[]{:S(2)}) async-start(bf16[32,160,128]{2,1,0:T(8,128)(2,1)} %shard_map.75), calls=%async_computation.1 | async-start | bytes 2621440 | tf_op jit(solution)/shard_map/all_to_all | solution.py:360
  162.2 15.9 %collective-permute-start.21 = (bf16[320,128]{1,0:T(8,128)(2,1)S(1)}, bf16[320,128]{1,0:T(8,128)(2,1)S(1)}, u32[]{:S(2)}, u32[]{:S(2)}) collective-permute-start(bf16[320,128]{1,0:T(8,128)(2,1)S(1)} %shard_map.76.here), channel_id=1, source_target_pairs={{0,32},{1,33},{2,34},{3,35},{4,36},{5,37},{6,38},{7,39},{8,40},{9,... | collective-permute-start | bytes 245768 | tf_op jit(solution)/shard_map/ppermute | solution.py:318
  186.3 8.5 %collective-permute-start.25 = (bf16[1280,128]{1,0:T(8,128)(2,1)S(1)}, bf16[1280,128]{1,0:T(8,128)(2,1)S(1)}, u32[]{:S(2)}, u32[]{:S(2)}) collective-permute-start(bf16[1280,128]{1,0:T(8,128)(2,1)S(1)} %shard_map.78.refs_0_), channel_id=1, source_target_pairs={{0,64},{1,9},{2,66},{3,11},{4,68},{5,13},{6,70},{7,15},{8,72},{9,1... | collective-permute-start | bytes 983048 | tf_op jit(solution)/shard_map/ppermute | solution.py:318
  189.6 9.6 %collective-permute-start.27 = (bf16[1280,128]{1,0:T(8,128)(2,1)S(1)}, bf16[1280,128]{1,0:T(8,128)(2,1)S(1)}, u32[]{:S(2)}, u32[]{:S(2)}) collective-permute-start(bf16[1280,128]{1,0:T(8,128)(2,1)S(1)} %shard_map.78.refs_0_), channel_id=1, source_target_pairs={{0,128},{1,17},{2,130},{3,19},{4,132},{5,21},{6,134},{7,23},{8,136... | collective-permute-start | bytes 983048 | tf_op jit(solution)/shard_map/ppermute | solution.py:318
  (31 other events, 97.6 us)
